TPU v7x, 1024 devices: a whole 4x8x16 slice. The times are simulated.
1024 devices in a mesh: dp: 32 (over z, core), expert: 32 (over y, x).
Axes of the slice: x: 4, y: 8, z: 16, core: 2. Of those that a mesh axis runs over, the one named last changes fastest.
Arguments:
- tokens: bfloat16 [262144, 1024], P(('dp', 'expert')), may hold values from -6 to 6
- router: bfloat16 [1024, 32], replicated, may hold values from -0.1875 to 0.1875
- w_in: bfloat16 [32, 1024, 2048], P('expert'), may hold values from -0.1875 to 0.1875
- w_out: bfloat16 [32, 2048, 1024], P('expert'), may hold values from -0.125 to 0.125
- assign: int32 [262144], P(('dp', 'expert')), may hold values from 0 to 31, as said below
- modality: int32 [262144], P(('dp', 'expert')), may hold values from 0 to 1
- slot: int32 [262144], P(('dp', 'expert')), may hold values from 0 to 11, as said below
Outputs:
- mixed: bfloat16 [262144, 1024], P(('dp', 'expert'))
- importance: float32 [2, 32], replicated
- entropies: float32 [2, 2], replicated
Inputs may be any that keep to these rules, and one draw needn't show every extreme that they name: `assign`: in the rows of one device each expert is named at most 12 times; in every device's rows one expert is named exactly 12 times, the same expert for all devices of one index of dp. A token's slot is the number of earlier rows of the same device that name the same expert.
All inputs are finite; a program needn't handle non-finite values.
Results may differ from a plain program's by a relative error of at most 0.003.
The roundings to bfloat16 on the way count: a program that leaves them out, or rounds other values in their place, can miss the bound.
Values may be sent and summed in bfloat16 or wider, within the bound.
No kernel may reach another device: no remote copies, remote signals or barrier semaphores. Data moves between devices by JAX's collectives and lax.ppermute only.
A program may use at most 32 MiB of HBM per device.

v0:
```python
import jax
import jax.numpy as jnp
from jax import lax
from jax.sharding import Mesh
from jax.sharding import PartitionSpec as P

DP = ("dp_0", "dp_1")
DP_EXPERT = ("dp_0", "dp_1", "expert")


def sent_to_all(x, axis):
    copies = jnp.broadcast_to(x, (lax.axis_size(axis), *x.shape))
    return lax.all_to_all(copies, axis, split_axis=0, concat_axis=0, tiled=True)


def over_copies(x, axis):
    everything = sent_to_all(x, axis)
    return jnp.sum(everything, axis=0)


def in_one(arrays, axis):
    ends = [0]
    for a in arrays:
        ends.append(ends[-1] + a.size)
    subtotal = over_copies(jnp.concatenate([a.ravel() for a in arrays]), axis)
    return tuple((subtotal[b:e].reshape(a.shape) for a, b, e in zip(arrays, ends, ends[1:])))


def one_axis_at_a_time(x, axes):
    for axis in axes:
        x = lax.psum(x, axis)
    return x


def local_statistics(probs, token_entropy, modality):
    kinds = (modality[:, None] == jnp.arange(2, dtype=jnp.int32)[None, :]).astype(jnp.float32)
    sums = jnp.dot(kinds.T, probs, precision=lax.Precision.HIGHEST)
    counts = jnp.sum(kinds, axis=0)
    ent_sum = jnp.dot(kinds.T, token_entropy, precision=lax.Precision.HIGHEST)
    return (sums, counts, ent_sum)


def reduce_statistics(parts):
    grouped = in_one((parts[0], parts[1], parts[2]), "expert")
    return (
        one_axis_at_a_time(grouped[0], DP),
        one_axis_at_a_time(grouped[1], DP),
        one_axis_at_a_time(grouped[2], DP),
    )


def per_device(tokens, router, w_in, w_out, assign, modality, slot):
    logits = jnp.dot(tokens, router, preferred_element_type=jnp.float32)
    probs = jax.nn.softmax(logits, axis=-1)
    logp = jax.nn.log_softmax(logits, axis=-1)
    n_expert = router.shape[1]
    slot_count = 3 * tokens.shape[0] // (2 * n_expert)
    picked = (assign[:, None] == jnp.arange(n_expert, dtype=jnp.int32)[None, :]).astype(jnp.float32)
    gate = jnp.sum(probs * picked, axis=-1)
    token_entropy = -jnp.sum(probs * logp, axis=-1)
    parts = local_statistics(probs, token_entropy, modality)
    labels = assign * slot_count + slot
    placing = (
        labels[None, :] == jnp.arange(n_expert * slot_count, dtype=jnp.int32)[:, None]
    ).astype(jnp.bfloat16)
    buffer = jnp.dot(placing, tokens, preferred_element_type=jnp.float32).astype(jnp.bfloat16)
    buffer = buffer.reshape(n_expert, slot_count, tokens.shape[1])
    first = w_in[0]
    second = w_out[0]
    received = lax.all_to_all(buffer, "expert", split_axis=0, concat_axis=0, tiled=True)
    sources, items, width = received.shape
    rows = received.reshape(sources * items, width)
    hidden = jax.nn.gelu(jnp.dot(rows, first, preferred_element_type=jnp.float32)).astype(
        jnp.bfloat16
    )
    result = jnp.dot(hidden, second, preferred_element_type=jnp.float32).astype(jnp.bfloat16)
    computed = result.reshape(sources, items, width)
    returned = lax.all_to_all(computed, "expert", split_axis=0, concat_axis=0, tiled=True)
    flat = returned.reshape(n_expert * slot_count, tokens.shape[1])
    chosen = jnp.dot(placing.T, flat, preferred_element_type=jnp.float32)
    mixed = (gate[:, None] * chosen).astype(jnp.bfloat16)
    totals = reduce_statistics(parts)
    sums, counts, ent_sum = totals
    denom = jnp.maximum(counts, 1.0)
    importance = sums / denom[:, None]
    global_ent = -jnp.sum(jax.scipy.special.xlogy(importance, importance), axis=-1)
    entropies = jnp.stack([ent_sum / denom, global_ent], axis=1)
    return (mixed, importance, entropies)


def solution(mesh):
    finer = Mesh(mesh.devices.reshape(16, 2, mesh.shape["expert"]), ("dp_0", "dp_1", "expert"))
    placed = (
        P(DP_EXPERT, None),
        P(),
        P("expert", None, None),
        P("expert", None, None),
        P(DP_EXPERT),
        P(DP_EXPERT),
        P(DP_EXPERT),
    )
    return jax.shard_map(
        per_device,
        mesh=finer,
        in_specs=placed,
        out_specs=(P(DP_EXPERT, None), P(), P()),
        check_vma=False,
    )
```

profile of v0, /device:TPU:1, one launch (start us, length us, event | category | flops | bytes accessed | tf_op | source)
XLA Modules:
  0.0 115.7 jit_solution(14751774474939515672)
XLA Ops:
  0.7 0.8 multiply_add_fusion
  1.4 0.3 copy-done
  1.7 0.4 convolution_convert_fusion
  2.1 1.2 %reshape.47 = bf16[32,12,1024]{2,1,0:T(8,128)(2,1)} reshape(bf16[384,1024]{1,0:T(8,128)(2,1)S(1)} %convolution_convert_fusion) | data formatting | bytes 1572864 | tf_op jit(solution)/shard_map/reshape | solution.py:67
  3.3 10.5 %all-to-all-start = ((bf16[32,12,1024]{2,1,0:T(8,128)(2,1)}), bf16[32,12,1024]{2,1,0:T(8,128)(2,1)S(1)}, u32[]{:S(2)}, u32[]{:S(2)}) async-start(bf16[32,12,1024]{2,1,0:T(8,128)(2,1)} %reshape.47), calls=%async_computation | async-start | bytes 2097152 | tf_op jit(solution)/shard_map/all_to_all | solution.py:70
  13.8 0.3 fusion.33
  14.2 0.1 fusion.24
  14.4 0.1 convert_reduce_fusion
  14.5 0.1 convolution_bitcast_fusion
  14.7 19.4 %all-to-all-done = bf16[32,12,1024]{2,1,0:T(8,128)(2,1)S(1)} async-done(((bf16[32,12,1024]{2,1,0:T(8,128)(2,1)}), bf16[32,12,1024]{2,1,0:T(8,128)(2,1)S(1)}, u32[]{:S(2)}, u32[]{:S(2)}) %all-to-all-start) | async-done | bytes 786464 | tf_op jit(solution)/shard_map/all_to_all | solution.py:70
  34.1 0.6 broadcast_in_dim.6
  34.7 6.8 %all-to-all-start.2 = ((f32[32,1,68]{2,1,0:T(1,128)}), f32[32,1,68]{2,1,0:T(1,128)S(1)}, u32[]{:S(2)}, u32[]{:S(2)}) async-start(f32[32,1,68]{2,1,0:T(1,128)} %broadcast_in_dim.6), calls=%async_computation.2 | async-start | bytes 32768 | tf_op jit(solution)/shard_map/all_to_all | solution.py:13
  41.5 0.2 reshape.48
  41.7 7.1 %fusion.14 = bf16[384,1024]{1,0:T(8,128)(2,1)S(1)} fusion(bf16[1,2048,1024]{2,1,0:T(8,128)(2,1)} %param.10, bf16[384,1024]{1,0:T(8,128)(2,1)S(1)} %reshape.48, bf16[1,1024,2048]{2,1,0:T(8,128)(2,1)} %param.9), kind=kOutput, calls=%fused_computation.13 | convolution fusion | flops 3228696576 | bytes 9961472 | tf_op jit(solution)/shard_map/dot_general | solution.py:76
  48.7 1.2 %reshape.49 = bf16[32,12,1024]{2,1,0:T(8,128)(2,1)} reshape(bf16[384,1024]{1,0:T(8,128)(2,1)S(1)} %fusion.14) | data formatting | bytes 1572864 | tf_op jit(solution)/shard_map/reshape | solution.py:77
  49.9 0.1 all-to-all-done.2
  50.0 9.1 %all-to-all-start.1 = ((bf16[32,12,1024]{2,1,0:T(8,128)(2,1)}), bf16[32,12,1024]{2,1,0:T(8,128)(2,1)S(1)}, u32[]{:S(2)}, u32[]{:S(2)}) async-start(bf16[32,12,1024]{2,1,0:T(8,128)(2,1)} %reshape.49), calls=%async_computation.1 | async-start | bytes 2097152 | tf_op jit(solution)/shard_map/all_to_all | solution.py:78
  59.1 0.1 reshape.52
  59.3 42.7 %all-reduce = (f32[2,32]{1,0:T(2,128)S(1)}, f32[2]{0:T(128)S(1)}, f32[2]{0:T(128)S(1)}) all-reduce(f32[2,32]{1,0:T(2,128)S(1)} %reshape.52, f32[2]{0:T(128)S(1)} %get-tuple-element.28, f32[2]{0:T(128)S(1)} %get-tuple-element.27), channel_id=1, replica_groups=mesh['dp_0'=16,'dp_1'=2,'expert'=32] {'dp_0'}, use_global_device_ids=true, to_apply=%region_6.7 | all-reduce | flops 68 | bytes 544 | tf_op jit(solution)/shard_map/psum | solution.py:31
  102.0 10.8 %all-reduce.1 = (f32[2,32]{1,0:T(2,128)S(1)}, f32[2]{0:T(128)S(1)}, f32[2]{0:T(128)S(1)}) all-reduce(f32[2,32]{1,0:T(2,128)S(1)} %get-tuple-element.17, f32[2]{0:T(128)S(1)} %get-tuple-element.18, f32[2]{0:T(128)S(1)} %get-tuple-element.19), channel_id=1, replica_groups=mesh['dp_0'=16,'dp_1'=2,'expert'=32] {'dp_1'}, use_global_device_ids=true, to_apply=%region_7.8 | all-reduce | flops 68 | bytes 544 | tf_op jit(solution)/shard_map/psum | solution.py:31
  112.8 0.8 fusion.27
  113.6 0.7 copy.14
  114.2 0.2 reshape.50
  114.4 1.3 %fusion.17 = bf16[256,1024]{1,0:T(8,128)(2,1)} fusion(bf16[384,1024]{1,0:T(8,128)(2,1)S(1)} %reshape.50, f32[256]{0:T(256)S(1)} %get-tuple-element.16, s32[256]{0:T(256)S(1)} %multiply_add_fusion), kind=kOutput, calls=%fused_computation.16 | convolution fusion | flops 201949184 | bytes 1312768 | tf_op jit(solution)/shard_map/dot_general | solution.py:80
  (19 shorter events, 0.4 us)
Async XLA Ops:
  0.6 1.1 copy-start
  0.6 13.5 %copy-start.2 = (s32[256]{0:T(256)S(1)}, s32[256]{0:T(256)}, u32[]{:S(2)}) copy-start(s32[256]{0:T(256)} %param.11) | copy-start | bytes 3076
  0.7 13.1 %copy-start.1 = (bf16[1024,32]{0,1:T(8,128)(2,1)S(1)}, bf16[1024,32]{0,1:T(8,128)(2,1)}, u32[]{:S(2)}) copy-start(bf16[1024,32]{0,1:T(8,128)(2,1)} %param.8) | copy-start | bytes 196612
  0.7 13.5 %copy-start.3 = (s32[256]{0:T(256)S(1)}, s32[256]{0:T(256)}, u32[]{:S(2)}) copy-start(s32[256]{0:T(256)} %param.12) | copy-start | bytes 3076
  3.3 30.8 %all-to-all-start = ((bf16[32,12,1024]{2,1,0:T(8,128)(2,1)}), bf16[32,12,1024]{2,1,0:T(8,128)(2,1)S(1)}, u32[]{:S(2)}, u32[]{:S(2)}) async-start(bf16[32,12,1024]{2,1,0:T(8,128)(2,1)} %reshape.47), calls=%async_computation | async-start | bytes 2097152 | tf_op jit(solution)/shard_map/all_to_all | solution.py:70
  34.7 15.3 %all-to-all-start.2 = ((f32[32,1,68]{2,1,0:T(1,128)}), f32[32,1,68]{2,1,0:T(1,128)S(1)}, u32[]{:S(2)}, u32[]{:S(2)}) async-start(f32[32,1,68]{2,1,0:T(1,128)} %broadcast_in_dim.6), calls=%async_computation.2 | async-start | bytes 32768 | tf_op jit(solution)/shard_map/all_to_all | solution.py:13
  50.0 64.2 %all-to-all-start.1 = ((bf16[32,12,1024]{2,1,0:T(8,128)(2,1)}), bf16[32,12,1024]{2,1,0:T(8,128)(2,1)S(1)}, u32[]{:S(2)}, u32[]{:S(2)}) async-start(bf16[32,12,1024]{2,1,0:T(8,128)(2,1)} %reshape.49), calls=%async_computation.1 | async-start | bytes 2097152 | tf_op jit(solution)/shard_map/all_to_all | solution.py:78
where the time goes:
time: 116 us
  blocking collectives  53.5 us (46%)
  starting transfers between devices  26.3 us (23%)
  waiting for transfers between devices  19.5 us (17%)
  matrix products  9.25 us (8%)
  local copies, waits for them, and re-layouts  4.51 us (4%)
  other arithmetic  1.85 us (2%)
    psum x2, blocking collectives, one_axis_at_a_time(): x = lax.psum(x, axis)  53.5 us
    all_to_all x1, waiting for transfers between devices, per_device(): lax.all_to_all(buffer, 'expert', split_axis=0, concat_axis=0, tiled=True)  19.4 us
    all_to_all x1, starting transfers between devices, per_device(): lax.all_to_all(buffer, 'expert', split_axis=0, concat_axis=0, tiled=True)  10.5 us
    all_to_all x1, starting transfers between devices, per_device(): lax.all_to_all(computed, 'expert', split_axis=0, concat_axis=0, tiled=True)  9.09 us
    dot_general x1, matrix products, per_device(): jnp.dot(hidden, second, preferred_element_type=jnp.float32)  7.06 us
    all_to_all x1, starting transfers between devices, sent_to_all(): return lax.all_to_all(copies, axis, split_axis=0, concat_axis=0, tiled=True)  6.75 us
  transfers between devices with their start and end apart: 3, of which 2 were waited for; matrix products, arithmetic and copies ran while one was open for 9% of the time, Pallas kernels for 0%

commit v1 on v0

v1 whole, which is shorter than its diff:
```python
import jax
import jax.numpy as jnp
from jax import lax
from jax.experimental import pallas as pl
from jax.experimental.pallas import tpu as pltpu
from jax.sharding import PartitionSpec as P

BOTH = ("dp", "expert")
F32, BF16, I32 = jnp.float32, jnp.bfloat16, jnp.int32
LANES = 128
ROWS = 8


def mm(a, b):
    return jnp.dot(a, b, preferred_element_type=F32)


def mm_t(a, b):
    return lax.dot_general(a, b, (((1,), (1,)), ((), ())), preferred_element_type=F32)


def iota(shape, dim):
    return lax.broadcasted_iota(I32, shape, dim)


def pick_labels(expert, slot):
    first = jnp.where(slot < 8, expert * 8 + slot, -1)
    low = jnp.where(slot >= 8, expert * 8 + slot - 8, -1)
    high = jnp.where(slot >= 8, expert * 8 + slot - 4, -1)
    return first, low, high


def gather_kernel(tokens, assign, slot, out):
    n_expert = out.shape[0]
    half = tokens.shape[1] // 2
    rows = n_expert * ROWS
    count = tokens.shape[0]
    experts = assign[...].reshape(1, count)
    slots = slot[...].reshape(1, count)
    first, low, high = pick_labels(experts, slots)
    row = iota((rows, count), 0)
    main = mm((first == row).astype(BF16), tokens[...]).astype(BF16)
    rest = mm((low == row).astype(BF16), tokens[:, :half])
    rest = rest + mm((high == row).astype(BF16), tokens[:, half:])
    rest = rest.astype(BF16)
    for t in range(8):
        out[:, t] = main[:, t * LANES : (t + 1) * LANES].reshape(n_expert, ROWS, LANES)
    for t in range(4):
        out[:, 8 + t] = rest[:, t * LANES : (t + 1) * LANES].reshape(n_expert, ROWS, LANES)


def split3(x):
    hi = x.astype(BF16)
    left = x - hi.astype(F32)
    mid = left.astype(BF16)
    lo = (left - mid.astype(F32)).astype(BF16)
    return hi, mid, lo


def column(row, count):
    return jnp.transpose(jnp.broadcast_to(row, (LANES, count)))


def stats_kernel(tokens, router_t, assign, modality, slot, stats, gate_out, place_first, place_low, place_high):
    n_expert, count = router_t.shape[0], tokens.shape[0]
    logits = mm_t(router_t[...], tokens[...])
    shifted = logits - jnp.max(logits, axis=0, keepdims=True)
    grown = jnp.exp(shifted)
    total = jnp.sum(grown, axis=0, keepdims=True)
    probs = grown / total
    logp = shifted - jnp.log(total)
    entropy = -jnp.sum(probs * logp, axis=0, keepdims=True)
    experts = assign[...].reshape(1, count)
    slots = slot[...].reshape(1, count)
    gate = jnp.sum(jnp.where(iota((n_expert, count), 0) == experts, probs, 0.0), axis=0, keepdims=True)
    r = iota((ROWS, count), 0)
    tail = jnp.where(r == 0, 1.0, jnp.where(r == 1, entropy, 0.0))
    pad = jnp.zeros((LANES - n_expert - ROWS, count), F32)
    terms = jnp.concatenate([probs, tail, pad], axis=0)
    kinds = (modality[...].reshape(1, count) == (iota((16, count), 0) & 1)).astype(BF16)
    hi, mid, lo = split3(terms)
    stats[...] = (mm_t(kinds, hi) + mm_t(kinds, mid) + mm_t(kinds, lo))[:ROWS]
    gate_out[...] = column(gate, count)
    wide = n_expert * ROWS
    first, low, high = pick_labels(experts, slots)
    lane = iota((count, wide), 1)

    def spread(labels):
        c = column(labels.astype(F32), count).astype(I32)
        return jnp.concatenate([c] * (wide // LANES), axis=1)

    place_first[...] = (spread(first) == lane).astype(BF16)
    place_low[...] = (spread(low) == lane).astype(BF16)
    place_high[...] = (spread(high) == lane).astype(BF16)


def ffn_kernel(received, w_in, w_out, stats, out, rows, acc):
    step = pl.program_id(0)
    n_expert = received.shape[0]
    wide = n_expert * ROWS
    quarter = wide // 2
    width = w_in.shape[1]
    half = width // 2

    @pl.when(step == 0)
    def _():
        for t in range(8):
            rows[:wide, t * LANES : (t + 1) * LANES] = received[:, t].reshape(wide, LANES)
        packed = jnp.concatenate([received[:, 8 + t].reshape(wide, LANES) for t in range(4)], axis=1)
        want = iota((quarter, wide), 0)
        have = iota((quarter, wide), 1)
        source = (want // 4) * 8 + want % 4
        rows[wide:, :half] = mm((have == source).astype(BF16), packed).astype(BF16)
        rows[wide:, half:] = mm((have == source + 4).astype(BF16), packed).astype(BF16)

    hidden = jax.nn.gelu(mm(rows[...], w_in[0])).astype(BF16)
    part = mm(hidden, w_out[0])

    @pl.when(step == 0)
    def _():
        acc[...] = part

    @pl.when(step > 0)
    def _():
        acc[...] = acc[...] + part

    @pl.when(step == pl.num_programs(0) - 1)
    def _():
        result = acc[...].astype(BF16)
        for t in range(8):
            out[:, t] = result[:wide, t * LANES : (t + 1) * LANES].reshape(n_expert, ROWS, LANES)
        want = iota((wide, quarter), 0)
        have = iota((wide, quarter), 1)
        inside = want % 8
        base = (want // 8) * 4
        low = jnp.where((inside < 4) & (have == base + inside), 1.0, 0.0).astype(BF16)
        high = jnp.where((inside >= 4) & (have == base + inside - 4), 1.0, 0.0).astype(BF16)
        packed = (mm(low, result[wide:, :half]) + mm(high, result[wide:, half:])).astype(BF16)
        for t in range(4):
            out[:, 8 + t] = packed[:, t * LANES : (t + 1) * LANES].reshape(n_expert, ROWS, LANES)
        hi, mid, lo = (p.astype(F32) for p in split3(stats[...]))
        r = iota((ROWS, LANES), 0)
        tile = jnp.where(r < 2, hi, jnp.where(r < 4, mid, jnp.where(r < 6, lo, 0.0))).astype(BF16)
        out[:, 12] = jnp.broadcast_to(tile[None], (n_expert, ROWS, LANES))


def mix_kernel(returned, gate, place_first, place_low, place_high, mixed, importance, entropies):
    n_expert = returned.shape[0]
    wide = n_expert * ROWS
    width = mixed.shape[1]
    half = width // 2
    scale = gate[...]
    scale = jnp.concatenate([scale] * (half // LANES), axis=1)
    main = jnp.concatenate([returned[:, t].reshape(wide, LANES) for t in range(8)], axis=1)
    packed = jnp.concatenate([returned[:, 8 + t].reshape(wide, LANES) for t in range(4)], axis=1)
    chosen = mm(place_first[...], main[:, :half]) + mm(place_low[...], packed)
    mixed[:, :half] = (scale * chosen).astype(BF16)
    chosen = mm(place_first[...], main[:, half:]) + mm(place_high[...], packed)
    mixed[:, half:] = (scale * chosen).astype(BF16)
    tile = jnp.sum(returned[:, 12].astype(F32), axis=0)
    total = (tile[0:2] + tile[2:4]) + tile[4:6]
    denom = jnp.maximum(total[:, n_expert : n_expert + 1], 1.0)
    mean = total[:, :n_expert] / denom
    importance[...] = mean
    terms = jnp.where(mean == 0.0, 0.0, mean * jnp.log(jnp.where(mean == 0.0, 1.0, mean)))
    spread = -jnp.sum(terms, axis=1, keepdims=True)
    token = total[:, n_expert + 1 : n_expert + 2] / denom
    entropies[...] = jnp.where(iota((2, 2), 1) == 0, token, spread)


def budget(mib):
    return pltpu.CompilerParams(vmem_limit_bytes=mib * 1024 * 1024)


def out_of(shape, dtype):
    return jax.ShapeDtypeStruct(shape, dtype)


def per_device(tokens, router, w_in, w_out, assign, modality, slot):
    count, width = tokens.shape
    n_expert = router.shape[1]
    hidden_width = w_in.shape[2]
    wide = n_expert * ROWS
    tiles = width // LANES * 3 // 2
    n_dp = lax.axis_size("dp")
    buffer = pl.pallas_call(
        gather_kernel, out_shape=out_of((n_expert, tiles, ROWS, LANES), BF16), name="gather", compiler_params=budget(24)
    )(tokens, assign, slot)
    received = lax.all_to_all(buffer, "expert", split_axis=0, concat_axis=0, tiled=True)
    stats, gate, place_first, place_low, place_high = pl.pallas_call(
        stats_kernel,
        out_shape=(
            out_of((ROWS, LANES), F32),
            out_of((count, LANES), F32),
            out_of((count, wide), BF16),
            out_of((count, wide), BF16),
            out_of((count, wide), BF16),
        ),
        name="stats",
        compiler_params=budget(24),
    )(tokens, router.T, assign, modality, slot)
    pairs = [[2 * z, 2 * z + 1] for z in range(n_dp // 2)]
    near = [[8 * j + 2 * z + c for z in range(4)] for j in range(n_dp // 8) for c in range(2)]
    far = [[8 * j + 2 * z + c for j in range(n_dp // 8)] for z in range(4) for c in range(2)]
    for groups in (pairs, near, far):
        stats = lax.psum(stats, "dp", axis_index_groups=groups)
    block = 256
    returned_in = pl.pallas_call(
        ffn_kernel,
        grid=(hidden_width // block,),
        in_specs=[
            pl.BlockSpec((n_expert, tiles, ROWS, LANES), lambda j: (0, 0, 0, 0)),
            pl.BlockSpec((1, width, block), lambda j: (0, 0, j)),
            pl.BlockSpec((1, block, width), lambda j: (0, j, 0)),
            pl.BlockSpec((ROWS, LANES), lambda j: (0, 0)),
        ],
        out_specs=pl.BlockSpec((n_expert, tiles + 1, ROWS, LANES), lambda j: (0, 0, 0, 0)),
        out_shape=out_of((n_expert, tiles + 1, ROWS, LANES), BF16),
        scratch_shapes=[
            pltpu.VMEM((wide * 3 // 2, width), BF16),
            pltpu.VMEM((wide * 3 // 2, width), F32),
        ],
        name="ffn",
        compiler_params=budget(60),
    )(received, w_in, w_out, stats)
    returned = lax.all_to_all(returned_in, "expert", split_axis=0, concat_axis=0, tiled=True)
    return pl.pallas_call(
        mix_kernel,
        out_shape=(
            out_of((count, width), BF16),
            out_of((2, n_expert), F32),
            out_of((2, 2), F32),
        ),
        name="mix",
        compiler_params=budget(24),
    )(returned, gate, place_first, place_low, place_high)


def solution(mesh):
    placed = (
        P(BOTH, None),
        P(),
        P("expert", None, None),
        P("expert", None, None),
        P(BOTH),
        P(BOTH),
        P(BOTH),
    )
    return jax.shard_map(
        per_device,
        mesh=mesh,
        in_specs=placed,
        out_specs=(P(BOTH, None), P(), P()),
        check_vma=False,
    )
```

time: 116 us -> 106 us (0.914)
  the two profiles are of different devices: /device:TPU:1 before, /device:TPU:2 now
where the time goes in v1:
time: 106 us
  blocking collectives  65.3 us (62%)
  starting transfers between devices  16.7 us (16%)
  Pallas kernels  15.6 us (15%)
  local copies, waits for them, and re-layouts  7.21 us (7%)
    psum x3, blocking collectives, per_device(): stats = lax.psum(stats, 'dp', axis_index_groups=groups)  34.9 us
    all_to_all x1, blocking collectives, per_device(): lax.all_to_all(returned_in, 'expert', split_axis=0, concat_axis=0, tiled=...  30.4 us
    all_to_all x1, starting transfers between devices, per_device(): lax.all_to_all(buffer, 'expert', split_axis=0, concat_axis=0, tiled=True)  16.7 us
    pallas_call x1, Pallas kernels, per_device(): pl.pallas_call(ffn_kernel, grid=(hidden_width // block,), in_specs=[pl.Bl...  12.5 us
    unnamed x18, local copies, waits for them, and re-layouts  7.21 us
  transfers between devices with their start and end apart: 1, of which 0 were waited for; matrix products, arithmetic and copies ran while one was open for 0% of the time, Pallas kernels for 1%

profile of v1, /device:TPU:2, one launch (start us, length us, event | category | flops | bytes accessed | tf_op | source)
XLA Modules:
  0.0 105.6 jit_solution(7449923510491615037)
XLA Ops:
  0.6 0.0 copy-start
  0.6 1.0 copy-done
  1.7 0.0 copy-start.3
  1.7 0.7 copy-done.3
  2.4 0.0 copy-start.5
  2.4 0.7 copy-done.5
  3.0 1.3 %gather.1 = bf16[32,12,8,128]{3,2,1,0:T(8,128)(2,1)} custom-call(bf16[256,1024]{1,0:T(8,128)(2,1)S(1)} %copy-done, s32[256]{0:T(256)S(1)} %copy-done.3, s32[256]{0:T(256)S(1)} %copy-done.5), custom_call_target="tpu_custom_call" | custom-call | tf_op jit(solution)/shard_map/gather/pallas_call | solution.py:186
  4.4 16.7 %all-to-all-start = ((bf16[32,12,8,128]{3,2,1,0:T(8,128)(2,1)}), bf16[32,12,8,128]{3,2,1,0:T(8,128)(2,1)S(1)}, u32[]{:S(2)}, u32[]{:S(2)}) async-start(bf16[32,12,8,128]{3,2,1,0:T(8,128)(2,1)} %gather.1), calls=%async_computation | async-start | bytes 1572864 | tf_op jit(solution)/shard_map/all_to_all | solution.py:189
  21.1 0.0 copy-start.1
  21.1 1.0 copy-done.1
  22.1 0.0 copy-start.2
  22.1 0.8 copy-done.2
  23.0 0.7 copy-done.4
  23.7 0.7 copy-done.6
  24.3 0.7 copy-done.7
  25.0 0.6 stats.1
  25.6 2.4 %psum.21 = f32[8,128]{1,0:T(8,128)S(1)} all-reduce(f32[8,128]{1,0:T(8,128)S(1)} %get-tuple-element.8), channel_id=1, replica_groups={{0,32},{64,96},{128,160},{192,224},{256,288},{320,352},{384,416},{448,4..., use_global_device_ids=true, to_apply=%region_0.0 | all-reduce | flops 1024 | bytes 8192 | tf_op jit(solution)/shard_map/psum | solution.py:206
  28.0 8.3 %psum.22 = f32[8,128]{1,0:T(8,128)S(1)} all-reduce(f32[8,128]{1,0:T(8,128)S(1)} %psum.21), channel_id=1, replica_groups={{0,64,128,192},{32,96,160,224},{256,320,384,448},{288,352,416,480},{512..., use_global_device_ids=true, to_apply=%region_1.0 | all-reduce | flops 1024 | bytes 8192 | tf_op jit(solution)/shard_map/psum | solution.py:206
  36.4 24.1 %psum.23.stats = f32[8,128]{1,0:T(8,128)} all-reduce(f32[8,128]{1,0:T(8,128)S(1)} %psum.22), channel_id=1, replica_groups={{0,256,512,768},{32,288,544,800},{64,320,576,832},{96,352,608,864},{128..., use_global_device_ids=true, to_apply=%region_2.0 | all-reduce | flops 1024 | bytes 8192 | tf_op jit(solution)/shard_map/psum | solution.py:206
  60.5 0.0 all-to-all-done.received
  60.5 0.9 copy-done.8
  61.4 12.5 %ffn.1 = bf16[32,13,8,128]{3,2,1,0:T(8,128)(2,1)} custom-call(bf16[32,12,8,128]{3,2,1,0:T(8,128)(2,1)} %copy-done.8, bf16[1,1024,2048]{2,1,0:T(8,128)(2,1)} %w_in.1, bf16[1,2048,1024]{2,1,0:T(8,128)(2,1)} %w_out.1, f32[8,128]{1,0:T(8,128)} %psum.23.stats), custom_call_target="tpu_custom_call" | custom-call | tf_op jit(solution)/shard_map/ffn/pallas_call | solution.py:208
  73.9 30.4 %all_to_all.10.returned = bf16[32,13,8,128]{3,2,1,0:T(8,128)(2,1)S(1)} all-to-all(bf16[32,13,8,128]{3,2,1,0:T(8,128)(2,1)} %ffn.1), channel_id=1, replica_groups=mesh['dp'=32,'expert'=32] {'expert'}, dimensions={0} | all-to-all | bytes 1703936 | tf_op jit(solution)/shard_map/all_to_all | solution.py:226
  104.3 1.2 %mix.1 = (bf16[256,1024]{1,0:T(8,128)(2,1)}, f32[2,32]{1,0:T(2,128)}, f32[2,2]{1,0:T(2,128)}) custom-call(bf16[32,13,8,128]{3,2,1,0:T(8,128)(2,1)S(1)} %all_to_all.10.returned, f32[256,128]{1,0:T(8,128)S(1)} %get-tuple-element.9.gate, bf16[256,256]{1,0:T(8,128)(2,1)S(1)} %get-tuple-element.10.place_first, bf16[256,256]{1,0:T(8,128)(2,1)S(1)} %get-tuple-element.11.place_low, ...), custom_call_target="tpu_custom_call" | custom-call | tf_op jit(solution)/shard_map/mix/pallas_call | solution.py:227
  (4 shorter events, 0.0 us)
Async XLA Ops:
  0.6 1.0 copy-start
  1.7 0.7 copy-start.3
  2.4 0.7 copy-start.5
  4.4 56.1 %all-to-all-start = ((bf16[32,12,8,128]{3,2,1,0:T(8,128)(2,1)}), bf16[32,12,8,128]{3,2,1,0:T(8,128)(2,1)S(1)}, u32[]{:S(2)}, u32[]{:S(2)}) async-start(bf16[32,12,8,128]{3,2,1,0:T(8,128)(2,1)} %gather.1), calls=%async_computation | async-start | bytes 1572864 | tf_op jit(solution)/shard_map/all_to_all | solution.py:189
  21.1 1.0 copy-start.1
  22.1 0.8 copy-start.2
  23.0 0.7 copy-start.4
  23.7 0.7 copy-start.6
  24.3 0.7 copy-start.7
  60.5 0.9 copy-start.8

commit v2 on v1

v2 whole, which is shorter than its diff:
```python
import jax
import jax.numpy as jnp
from jax import lax
from jax.experimental import pallas as pl
from jax.experimental.pallas import tpu as pltpu
from jax.sharding import PartitionSpec as P

BOTH = ("dp", "expert")
F32, BF16, I32 = jnp.float32, jnp.bfloat16, jnp.int32
LANES = 128
ROWS = 8


def mm(a, b):
    return jnp.dot(a, b, preferred_element_type=F32)


def mm_t(a, b):
    return lax.dot_general(a, b, (((1,), (1,)), ((), ())), preferred_element_type=F32)


def iota(shape, dim):
    return lax.broadcasted_iota(I32, shape, dim)


def pick_labels(expert, slot):
    first = jnp.where(slot < 8, expert * 8 + slot, -1)
    low = jnp.where(slot >= 8, expert * 8 + slot - 8, -1)
    high = jnp.where(slot >= 8, expert * 8 + slot - 4, -1)
    return first, low, high


def split3(x):
    hi = x.astype(BF16)
    left = x - hi.astype(F32)
    mid = left.astype(BF16)
    lo = (left - mid.astype(F32)).astype(BF16)
    return hi, mid, lo


def stats_tile(sums):
    hi, mid, lo = (p.astype(F32) for p in split3(sums))
    r = iota((ROWS, LANES), 0)
    return jnp.where(r < 2, hi, jnp.where(r < 4, mid, jnp.where(r < 6, lo, 0.0))).astype(BF16)


def fetch(sources, targets, sems):
    copies = [pltpu.make_async_copy(s, t, sems.at[i]) for i, (s, t) in enumerate(zip(sources, targets))]
    for c in copies:
        c.start()
    return copies


def send_kernel(
    tokens_hbm, router_hbm, assign_hbm, slot_hbm, modality_hbm, out, gate_out, tokens, router, assign, slot, modality, sems
):
    copies = fetch(
        (assign_hbm, slot_hbm, tokens_hbm, router_hbm, modality_hbm), (assign, slot, tokens, router, modality), sems
    )
    n_expert = out.shape[0]
    count, width = tokens.shape
    half = width // 2
    rows = n_expert * ROWS
    copies[0].wait()
    copies[1].wait()
    experts = assign[...].reshape(1, count)
    slots = slot[...].reshape(1, count)
    first, low, high = pick_labels(experts, slots)
    row = iota((rows, count), 0)
    pick_first = (first == row).astype(BF16)
    pick_low = (low == row).astype(BF16)
    pick_high = (high == row).astype(BF16)
    copies[2].wait()
    main = mm(pick_first, tokens[...]).astype(BF16)
    rest = mm(pick_low, tokens[:, :half]) + mm(pick_high, tokens[:, half:])
    rest = rest.astype(BF16)
    for t in range(8):
        out[:, t] = main[:, t * LANES : (t + 1) * LANES].reshape(n_expert, ROWS, LANES)
    for t in range(4):
        out[:, 8 + t] = rest[:, t * LANES : (t + 1) * LANES].reshape(n_expert, ROWS, LANES)
    copies[3].wait()
    copies[4].wait()
    logits = mm_t(router[...], tokens[...])
    shifted = logits - jnp.max(logits, axis=0, keepdims=True)
    grown = jnp.exp(shifted)
    total = jnp.sum(grown, axis=0, keepdims=True)
    probs = grown / total
    logp = shifted - jnp.log(total)
    entropy = -jnp.sum(probs * logp, axis=0, keepdims=True)
    gate = jnp.sum(jnp.where(iota((n_expert, count), 0) == experts, probs, 0.0), axis=0, keepdims=True)
    gate_out[...] = jnp.broadcast_to(gate, (ROWS, count))
    r = iota((ROWS, count), 0)
    tail = jnp.where(r == 0, 1.0, jnp.where(r == 1, entropy, 0.0))
    pad = jnp.zeros((LANES - n_expert - ROWS, count), F32)
    terms = jnp.concatenate([probs, tail, pad], axis=0)
    kinds = (modality[...].reshape(1, count) == (iota((16, count), 0) & 1)).astype(BF16)
    hi, mid, lo = split3(terms)
    sums = (mm_t(kinds, hi) + mm_t(kinds, mid) + mm_t(kinds, lo))[:ROWS]
    out[:, 12] = jnp.broadcast_to(stats_tile(sums)[None], (n_expert, ROWS, LANES))


def total_of(tiles):
    tile = jnp.sum(tiles.astype(F32), axis=0)
    return (tile[0:2] + tile[2:4]) + tile[4:6]


def group_kernel(received, group):
    total = total_of(received[:, 12])
    group[...] = jnp.concatenate([total] * (ROWS // 2), axis=0)


def fill_kernel(computed, other, out):
    n_expert = out.shape[0]
    out[:, 12] = jnp.broadcast_to(stats_tile(other[...])[None], (n_expert, ROWS, LANES))


def column(row, count):
    return jnp.transpose(jnp.broadcast_to(row, (LANES, count)))


def place_kernel(gate, assign, slot, after, gate_out, place_first, place_low, place_high):
    count = gate.shape[1]
    wide = place_first.shape[1]
    first, low, high = pick_labels(assign[...].reshape(1, count), slot[...].reshape(1, count))
    gate_out[...] = column(gate[0:1], count)
    lane = iota((count, wide), 1)

    def spread(labels):
        c = column(labels.astype(F32), count).astype(I32)
        return jnp.concatenate([c] * (wide // LANES), axis=1)

    place_first[...] = (spread(first) == lane).astype(BF16)
    place_low[...] = (spread(low) == lane).astype(BF16)
    place_high[...] = (spread(high) == lane).astype(BF16)


STEP = 256


def ffn_kernel(received, in_hbm, out_hbm, out, w_in, w_out, rows, hidden, rest, sems):
    n_expert = received.shape[0]
    wide = n_expert * ROWS
    quarter = wide // 2
    width, inner = w_in.shape
    half = width // 2
    n_in, n_out = inner // STEP, width // STEP
    order = [0, 2, 1, 3]
    cut = [pl.ds(j * STEP, STEP) for j in range(max(n_in, n_out))]
    copies = fetch(
        [in_hbm.at[0, :, cut[j]] for j in range(n_in)] + [out_hbm.at[0, :, cut[n]] for n in order],
        [w_in.at[:, cut[j]] for j in range(n_in)] + [w_out.at[:, cut[n]] for n in order],
        sems,
    )
    for t in range(8):
        rows[:wide, t * LANES : (t + 1) * LANES] = received[:, t].reshape(wide, LANES)
    packed = jnp.concatenate([received[:, 8 + t].reshape(wide, LANES) for t in range(4)], axis=1)
    want = iota((quarter, wide), 0)
    have = iota((quarter, wide), 1)
    source = (want // 4) * 8 + want % 4
    rows[wide:, :half] = mm((have == source).astype(BF16), packed).astype(BF16)
    rows[wide:, half:] = mm((have == source + 4).astype(BF16), packed).astype(BF16)
    for j in range(n_in):
        copies[j].wait()
        hidden[:, j * STEP : (j + 1) * STEP] = jax.nn.gelu(mm(rows[...], w_in[:, cut[j]])).astype(BF16)
    want = iota((wide, quarter), 0)
    have = iota((wide, quarter), 1)
    inside = want % 8
    base = (want // 8) * 4
    to_low = jnp.where((inside < 4) & (have == base + inside), 1.0, 0.0).astype(BF16)
    to_high = jnp.where((inside >= 4) & (have == base + inside - 4), 1.0, 0.0).astype(BF16)
    for i, n in enumerate(order):
        copies[n_in + i].wait()
        result = mm(hidden[...], w_out[:, cut[n]]).astype(BF16)
        for k in range(STEP // LANES):
            t = n * (STEP // LANES) + k
            out[:, t] = result[:wide, k * LANES : (k + 1) * LANES].reshape(n_expert, ROWS, LANES)
        rest[:, n * STEP : (n + 1) * STEP] = result[wide:]
        if i % 2 == 1:
            lo = order[i - 1]
            packed = mm(to_low, rest[:, lo * STEP : (lo + 1) * STEP]) + mm(to_high, rest[:, n * STEP : (n + 1) * STEP])
            packed = packed.astype(BF16)
            for k in range(STEP // LANES):
                t = 8 + lo * (STEP // LANES) + k
                out[:, t] = packed[:, k * LANES : (k + 1) * LANES].reshape(n_expert, ROWS, LANES)


def mix_kernel(returned, gate, place_first, place_low, place_high, mixed, importance, entropies):
    n_expert = returned.shape[0]
    wide = n_expert * ROWS
    width = mixed.shape[1]
    half = width // 2
    scale = gate[...]
    scale = jnp.concatenate([scale] * (half // LANES), axis=1)
    main = jnp.concatenate([returned[:, t].reshape(wide, LANES) for t in range(8)], axis=1)
    packed = jnp.concatenate([returned[:, 8 + t].reshape(wide, LANES) for t in range(4)], axis=1)
    chosen = mm(place_first[...], main[:, :half]) + mm(place_low[...], packed)
    mixed[:, :half] = (scale * chosen).astype(BF16)
    chosen = mm(place_first[...], main[:, half:]) + mm(place_high[...], packed)
    mixed[:, half:] = (scale * chosen).astype(BF16)
    total = total_of(returned[:, 12])
    denom = jnp.maximum(total[:, n_expert : n_expert + 1], 1.0)
    mean = total[:, :n_expert] / denom
    importance[...] = mean
    terms = jnp.where(mean == 0.0, 0.0, mean * jnp.log(jnp.where(mean == 0.0, 1.0, mean)))
    spread = -jnp.sum(terms, axis=1, keepdims=True)
    token = total[:, n_expert + 1 : n_expert + 2] / denom
    entropies[...] = jnp.where(iota((2, 2), 1) == 0, token, spread)


def budget(kib):
    return pltpu.CompilerParams(vmem_limit_bytes=kib * 1024)


def out_of(shape, dtype):
    return jax.ShapeDtypeStruct(shape, dtype)


HBM = pl.BlockSpec(memory_space=pltpu.HBM)
VMEM = pl.BlockSpec(memory_space=pltpu.VMEM)


def per_device(tokens, router, w_in, w_out, assign, modality, slot):
    count, width = tokens.shape
    n_expert = router.shape[1]
    inner = w_in.shape[2]
    wide = n_expert * ROWS
    tiles = width // LANES * 3 // 2
    n_dp = lax.axis_size("dp")
    block = out_of((n_expert, tiles + 1, ROWS, LANES), BF16)
    ints = pltpu.VMEM((count,), I32)
    buffer, gate = pl.pallas_call(
        send_kernel,
        in_specs=[HBM] * 5,
        out_specs=(VMEM, VMEM),
        out_shape=(block, out_of((ROWS, count), F32)),
        scratch_shapes=[
            pltpu.VMEM((count, width), BF16),
            pltpu.VMEM((n_expert, width), BF16),
            ints,
            ints,
            ints,
            pltpu.SemaphoreType.DMA((5,)),
        ],
        name="send",
        compiler_params=budget(65472),
    )(tokens, router.T, assign, slot, modality)
    received = lax.all_to_all(buffer, "expert", split_axis=0, concat_axis=0, tiled=True)
    group = pl.pallas_call(
        group_kernel, in_specs=[VMEM], out_specs=VMEM, out_shape=out_of((ROWS, LANES), F32), name="group",
        compiler_params=budget(24576),
    )(received)
    swap = [(d * n_expert + e, (d ^ e) * n_expert + e) for d in range(n_dp) for e in range(n_expert)]
    other = lax.ppermute(group, ("dp", "expert"), swap)
    computed = pl.pallas_call(
        ffn_kernel,
        in_specs=[VMEM, HBM, HBM],
        out_specs=VMEM,
        out_shape=block,
        scratch_shapes=[
            pltpu.VMEM((width, inner), BF16),
            pltpu.VMEM((inner, width), BF16),
            pltpu.VMEM((wide * 3 // 2, width), BF16),
            pltpu.VMEM((wide * 3 // 2, inner), BF16),
            pltpu.VMEM((wide // 2, width), BF16),
            pltpu.SemaphoreType.DMA((inner // STEP + width // STEP,)),
        ],
        name="ffn",
        compiler_params=budget(50000),
    )(received, w_in, w_out)
    scale, place_first, place_low, place_high = pl.pallas_call(
        place_kernel,
        in_specs=[VMEM] * 4,
        out_specs=(VMEM,) * 4,
        out_shape=(
            out_of((count, LANES), F32),
            out_of((count, wide), BF16),
            out_of((count, wide), BF16),
            out_of((count, wide), BF16),
        ),
        name="place",
        compiler_params=budget(24576),
    )(gate, assign, slot, group)
    filled = pl.pallas_call(
        fill_kernel,
        in_specs=[VMEM, VMEM],
        out_specs=VMEM,
        out_shape=block,
        input_output_aliases={0: 0},
        name="fill",
        compiler_params=budget(24576),
    )(computed, other)
    filled, scale, place_first, place_low, place_high = lax.optimization_barrier(
        (filled, scale, place_first, place_low, place_high)
    )
    returned = lax.all_to_all(filled, "expert", split_axis=0, concat_axis=0, tiled=True)
    return pl.pallas_call(
        mix_kernel,
        in_specs=[VMEM] * 5,
        out_specs=(VMEM,) * 3,
        out_shape=(
            out_of((count, width), BF16),
            out_of((2, n_expert), F32),
            out_of((2, 2), F32),
        ),
        name="mix",
        compiler_params=budget(24576),
    )(returned, scale, place_first, place_low, place_high)


def solution(mesh):
    placed = (
        P(BOTH, None),
        P(),
        P("expert", None, None),
        P("expert", None, None),
        P(BOTH),
        P(BOTH),
        P(BOTH),
    )
    return jax.shard_map(
        per_device,
        mesh=mesh,
        in_specs=placed,
        out_specs=(P(BOTH, None), P(), P()),
        check_vma=False,
    )
```

time: 106 us -> 100 us (0.943)
  blocking collectives: 65.3 us -> 80.2 us
  starting transfers between devices: 16.7 us -> 1.92 us
  local copies, waits for them, and re-layouts: 7.21 us -> 2.05 us
    all_to_all x1 -> x2, blocking collectives: 30.4 us -> 80.2 us  [the longest x1 46.1 us: per_device(): lax.all_to_all(filled, 'expert', split_axis=0, concat_axis=0, tiled=True)]
    psum x3 -> x0, blocking collectives: 34.9 us -> none  [per_device(): stats = lax.psum(stats, 'dp', axis_index_groups=groups)]
    all_to_all x1 -> x0, starting transfers between devices: 16.7 us -> none  [per_device(): lax.all_to_all(buffer, 'expert', split_axis=0, concat_axis=0, tiled=True)]
    unnamed x18 -> x6, local copies, waits for them, and re-layouts: 7.21 us -> 2.05 us
    ppermute x0 -> x1, starting transfers between devices: none -> 1.92 us  [per_device(): other = lax.ppermute(group, ('dp', 'expert'), swap)]
    pallas_call x4 -> x6, Pallas kernels: 15.6 us -> 15 us  [the longest x1 10.3 us: per_device(): pl.pallas_call(ffn_kernel, in_specs=[VMEM, HBM, HBM], out_specs=VMEM, out...]
  transfers between devices with their start and end apart: 1 -> 1, of which waited for: 0 -> 0; matrix products, arithmetic and copies ran while one was open for 0% -> 0% of each run, Pallas kernels for 1% -> 11%
where the time goes in v2:
time: 100 us; the launch traced here: 99.8 us
  blocking collectives  80.2 us (80%)
  Pallas kernels  15 us (15%)
  local copies, waits for them, and re-layouts  2.05 us (2%)
  starting transfers between devices  1.92 us (2%)
    all_to_all x1, blocking collectives, per_device(): lax.all_to_all(filled, 'expert', split_axis=0, concat_axis=0, tiled=True)  46.1 us
    all_to_all x1, blocking collectives, per_device(): lax.all_to_all(buffer, 'expert', split_axis=0, concat_axis=0, tiled=True)  34.1 us
    pallas_call x1, Pallas kernels, per_device(): pl.pallas_call(ffn_kernel, in_specs=[VMEM, HBM, HBM], out_specs=VMEM, out...  10.3 us
    pallas_call x1, Pallas kernels, per_device(): pl.pallas_call(send_kernel, in_specs=[HBM] * 5, out_specs=(VMEM, VMEM), o...  3.19 us
    unnamed x6, local copies, waits for them, and re-layouts  2.05 us
  transfers between devices with their start and end apart: 1, of which 0 were waited for; matrix products, arithmetic and copies ran while one was open for 0% of the time, Pallas kernels for 11%

profile of v2, /device:TPU:2, one launch (start us, length us, event | category | flops | bytes accessed | tf_op | source)
XLA Modules:
  0.0 99.8 jit_solution(8602266976269875923)
XLA Ops:
  0.6 3.2 %send.1 = (bf16[32,13,8,128]{3,2,1,0:T(8,128)(2,1)}, f32[8,256]{1,0:T(8,128)}) custom-call(bf16[256,1024]{1,0:T(8,128)(2,1)} %tokens_hbm.1, bf16[32,1024]{1,0:T(8,128)(2,1)} %bitcast.1, s32[256]{0:T(256)} %assign.1, s32[256]{0:T(256)} %slot.1, s32[256]{0:T(256)} %modality_hbm.1), custom_call_target="tpu_custom_call" | custom-call | tf_op jit(solution)/shard_map/send/pallas_call | solution.py:231
  3.8 34.1 %all_to_all.10.received = bf16[32,13,8,128]{3,2,1,0:T(8,128)(2,1)S(1)} all-to-all(bf16[32,13,8,128]{3,2,1,0:T(8,128)(2,1)} %get-tuple-element.14), channel_id=1, replica_groups=mesh['dp'=32,'expert'=32] {'expert'}, dimensions={0} | all-to-all | bytes 1703936 | tf_op jit(solution)/shard_map/all_to_all | solution.py:247
  38.0 1.9 %collective-permute-start = (f32[8,128]{1,0:T(8,128)S(1)}, f32[8,128]{1,0:T(8,128)S(1)}, u32[]{:S(2)}, u32[]{:S(2)}) collective-permute-start(f32[8,128]{1,0:T(8,128)S(1)} %group.1.after), channel_id=1, source_target_pairs={{0,0},{1,33},{2,66},{3,99},{4,132},{5,165},{6,198},{7,231},{8,264}... | collective-permute-start | bytes 12296 | tf_op jit(solution)/shard_map/ppermute | solution.py:253
  39.9 0.0 copy-start
  39.9 0.7 copy-done
  40.6 0.0 copy-start.1
  40.6 0.7 copy-done.1
  41.3 0.0 copy-start.2
  41.3 0.7 copy-done.2
  42.0 0.2 place.1
  42.2 10.3 %ffn.1.computed = bf16[32,13,8,128]{3,2,1,0:T(8,128)(2,1)S(1)} custom-call(bf16[32,13,8,128]{3,2,1,0:T(8,128)(2,1)S(1)} %all_to_all.10.received, bf16[1,1024,2048]{2,1,0:T(8,128)(2,1)} %in_hbm.1, bf16[1,2048,1024]{2,1,0:T(8,128)(2,1)} %out_hbm.1), custom_call_target="tpu_custom_call" | custom-call | tf_op jit(solution)/shard_map/ffn/pallas_call | solution.py:254
  52.5 0.0 collective-permute-done.other
  52.5 46.1 %all_to_all.11.returned = bf16[32,13,8,128]{3,2,1,0:T(8,128)(2,1)S(1)} all-to-all(bf16[32,13,8,128]{3,2,1,0:T(8,128)(2,1)S(1)} %fill.1), channel_id=1, replica_groups=mesh['dp'=32,'expert'=32] {'expert'}, dimensions={0} | all-to-all | bytes 1703936 | tf_op jit(solution)/shard_map/all_to_all | solution.py:295
  98.6 1.2 %mix.1 = (bf16[256,1024]{1,0:T(8,128)(2,1)}, f32[2,32]{1,0:T(2,128)}, f32[2,2]{1,0:T(2,128)}) custom-call(bf16[32,13,8,128]{3,2,1,0:T(8,128)(2,1)S(1)} %all_to_all.11.returned, f32[256,128]{1,0:T(8,128)S(1)} %get-tuple-element.21.gate, bf16[256,256]{1,0:T(8,128)(2,1)S(1)} %get-tuple-element.22.place_first, bf16[256,256]{1,0:T(8,128)(2,1)S(1)} %get-tuple-element.23.place_low, ...), custom_call_target="tpu_custom_call" | custom-call | tf_op jit(solution)/shard_map/mix/pallas_call | solution.py:296
  (2 shorter events, 0.1 us)
Async XLA Ops:
  38.0 14.5 %collective-permute-start = (f32[8,128]{1,0:T(8,128)S(1)}, f32[8,128]{1,0:T(8,128)S(1)}, u32[]{:S(2)}, u32[]{:S(2)}) collective-permute-start(f32[8,128]{1,0:T(8,128)S(1)} %group.1.after), channel_id=1, source_target_pairs={{0,0},{1,33},{2,66},{3,99},{4,132},{5,165},{6,198},{7,231},{8,264}... | collective-permute-start | bytes 12296 | tf_op jit(solution)/shard_map/ppermute | solution.py:253
  39.9 0.7 copy-start
  40.6 0.7 copy-start.1
  41.3 0.7 copy-start.2

commit v3 on v2

--- a/solution.py
+++ b/solution.py
@@ -104,25 +104,15 @@
     return (tile[0:2] + tile[2:4]) + tile[4:6]
 
 
-def group_kernel(received, group):
-    total = total_of(received[:, 12])
-    group[...] = jnp.concatenate([total] * (ROWS // 2), axis=0)
-
-
-def fill_kernel(computed, other, out):
-    n_expert = out.shape[0]
-    out[:, 12] = jnp.broadcast_to(stats_tile(other[...])[None], (n_expert, ROWS, LANES))
-
-
 def column(row, count):
     return jnp.transpose(jnp.broadcast_to(row, (LANES, count)))
 
 
-def place_kernel(gate, assign, slot, after, gate_out, place_first, place_low, place_high):
+def place_kernel(gate, assign, slot, scale, place_first, place_low, place_high):
     count = gate.shape[1]
     wide = place_first.shape[1]
     first, low, high = pick_labels(assign[...].reshape(1, count), slot[...].reshape(1, count))
-    gate_out[...] = column(gate[0:1], count)
+    scale[...] = column(gate[0:1], count)
     lane = iota((count, wide), 1)
 
     def spread(labels):
@@ -134,21 +124,20 @@
     place_high[...] = (spread(high) == lane).astype(BF16)
 
 
-STEP = 256
-
-
-def ffn_kernel(received, in_hbm, out_hbm, out, w_in, w_out, rows, hidden, rest, sems):
+STEP = 512
+
+
+def ffn_kernel(received, in_hbm, out_hbm, out, group, w_in, w_out, rows, hidden, rest, sems):
     n_expert = received.shape[0]
     wide = n_expert * ROWS
     quarter = wide // 2
     width, inner = w_in.shape
     half = width // 2
     n_in, n_out = inner // STEP, width // STEP
-    order = [0, 2, 1, 3]
     cut = [pl.ds(j * STEP, STEP) for j in range(max(n_in, n_out))]
     copies = fetch(
-        [in_hbm.at[0, :, cut[j]] for j in range(n_in)] + [out_hbm.at[0, :, cut[n]] for n in order],
-        [w_in.at[:, cut[j]] for j in range(n_in)] + [w_out.at[:, cut[n]] for n in order],
+        [in_hbm.at[0, :, cut[j]] for j in range(n_in)] + [out_hbm.at[0, :, cut[n]] for n in range(n_out)],
+        [w_in.at[:, cut[j]] for j in range(n_in)] + [w_out.at[:, cut[n]] for n in range(n_out)],
         sems,
     )
     for t in range(8):
@@ -159,32 +148,30 @@
     source = (want // 4) * 8 + want % 4
     rows[wide:, :half] = mm((have == source).astype(BF16), packed).astype(BF16)
     rows[wide:, half:] = mm((have == source + 4).astype(BF16), packed).astype(BF16)
+    total = total_of(received[:, 12])
+    group[...] = jnp.concatenate([total] * (ROWS // 2), axis=0)
     for j in range(n_in):
         copies[j].wait()
         hidden[:, j * STEP : (j + 1) * STEP] = jax.nn.gelu(mm(rows[...], w_in[:, cut[j]])).astype(BF16)
+    for n in range(n_out):
+        copies[n_in + n].wait()
+        result = mm(hidden[...], w_out[:, cut[n]]).astype(BF16)
+        for k in range(STEP // LANES):
+            t = n * (STEP // LANES) + k
+            out[:, t] = result[:wide, k * LANES : (k + 1) * LANES].reshape(n_expert, ROWS, LANES)
+        rest[:, n * STEP : (n + 1) * STEP] = result[wide:]
     want = iota((wide, quarter), 0)
     have = iota((wide, quarter), 1)
     inside = want % 8
     base = (want // 8) * 4
     to_low = jnp.where((inside < 4) & (have == base + inside), 1.0, 0.0).astype(BF16)
     to_high = jnp.where((inside >= 4) & (have == base + inside - 4), 1.0, 0.0).astype(BF16)
-    for i, n in enumerate(order):
-        copies[n_in + i].wait()
-        result = mm(hidden[...], w_out[:, cut[n]]).astype(BF16)
-        for k in range(STEP // LANES):
-            t = n * (STEP // LANES) + k
-            out[:, t] = result[:wide, k * LANES : (k + 1) * LANES].reshape(n_expert, ROWS, LANES)
-        rest[:, n * STEP : (n + 1) * STEP] = result[wide:]
-        if i % 2 == 1:
-            lo = order[i - 1]
-            packed = mm(to_low, rest[:, lo * STEP : (lo + 1) * STEP]) + mm(to_high, rest[:, n * STEP : (n + 1) * STEP])
-            packed = packed.astype(BF16)
-            for k in range(STEP // LANES):
-                t = 8 + lo * (STEP // LANES) + k
-                out[:, t] = packed[:, k * LANES : (k + 1) * LANES].reshape(n_expert, ROWS, LANES)
-
-
-def mix_kernel(returned, gate, place_first, place_low, place_high, mixed, importance, entropies):
+    packed = (mm(to_low, rest[:, :half]) + mm(to_high, rest[:, half:])).astype(BF16)
+    for t in range(4):
+        out[:, 8 + t] = packed[:, t * LANES : (t + 1) * LANES].reshape(n_expert, ROWS, LANES)
+
+
+def mix_kernel(returned, sums, gate, place_first, place_low, place_high, mixed, importance, entropies):
     n_expert = returned.shape[0]
     wide = n_expert * ROWS
     width = mixed.shape[1]
@@ -197,7 +184,7 @@
     mixed[:, :half] = (scale * chosen).astype(BF16)
     chosen = mm(place_first[...], main[:, half:]) + mm(place_high[...], packed)
     mixed[:, half:] = (scale * chosen).astype(BF16)
-    total = total_of(returned[:, 12])
+    total = sums[0:2]
     denom = jnp.maximum(total[:, n_expert : n_expert + 1], 1.0)
     mean = total[:, :n_expert] / denom
     importance[...] = mean
@@ -245,17 +232,23 @@
         compiler_params=budget(65472),
     )(tokens, router.T, assign, slot, modality)
     received = lax.all_to_all(buffer, "expert", split_axis=0, concat_axis=0, tiled=True)
-    group = pl.pallas_call(
-        group_kernel, in_specs=[VMEM], out_specs=VMEM, out_shape=out_of((ROWS, LANES), F32), name="group",
+    place = out_of((count, wide), BF16)
+    scale, place_first, place_low, place_high = pl.pallas_call(
+        place_kernel,
+        in_specs=[VMEM] * 3,
+        out_specs=(VMEM,) * 4,
+        out_shape=(out_of((count, LANES), F32), place, place, place),
+        name="place",
         compiler_params=budget(24576),
-    )(received)
-    swap = [(d * n_expert + e, (d ^ e) * n_expert + e) for d in range(n_dp) for e in range(n_expert)]
-    other = lax.ppermute(group, ("dp", "expert"), swap)
-    computed = pl.pallas_call(
+    )(gate, assign, slot)
+    received, scale, place_first, place_low, place_high = lax.optimization_barrier(
+        (received, scale, place_first, place_low, place_high)
+    )
+    computed, stats = pl.pallas_call(
         ffn_kernel,
         in_specs=[VMEM, HBM, HBM],
-        out_specs=VMEM,
-        out_shape=block,
+        out_specs=(VMEM, VMEM),
+        out_shape=(out_of((n_expert, tiles, ROWS, LANES), BF16), out_of((ROWS, LANES), F32)),
         scratch_shapes=[
             pltpu.VMEM((width, inner), BF16),
             pltpu.VMEM((inner, width), BF16),
@@ -267,35 +260,15 @@
         name="ffn",
         compiler_params=budget(50000),
     )(received, w_in, w_out)
-    scale, place_first, place_low, place_high = pl.pallas_call(
-        place_kernel,
-        in_specs=[VMEM] * 4,
-        out_specs=(VMEM,) * 4,
-        out_shape=(
-            out_of((count, LANES), F32),
-            out_of((count, wide), BF16),
-            out_of((count, wide), BF16),
-            out_of((count, wide), BF16),
-        ),
-        name="place",
-        compiler_params=budget(24576),
-    )(gate, assign, slot, group)
-    filled = pl.pallas_call(
-        fill_kernel,
-        in_specs=[VMEM, VMEM],
-        out_specs=VMEM,
-        out_shape=block,
-        input_output_aliases={0: 0},
-        name="fill",
-        compiler_params=budget(24576),
-    )(computed, other)
-    filled, scale, place_first, place_low, place_high = lax.optimization_barrier(
-        (filled, scale, place_first, place_low, place_high)
-    )
-    returned = lax.all_to_all(filled, "expert", split_axis=0, concat_axis=0, tiled=True)
+    returned = lax.all_to_all(computed, "expert", split_axis=0, concat_axis=0, tiled=True)
+    pairs = [[2 * z, 2 * z + 1] for z in range(n_dp // 2)]
+    near = [[8 * j + 2 * z + c for z in range(4)] for j in range(n_dp // 8) for c in range(2)]
+    far = [[8 * j + 2 * z + c for j in range(n_dp // 8)] for z in range(4) for c in range(2)]
+    for groups in (pairs, near, far):
+        stats = lax.psum(stats, "dp", axis_index_groups=groups)
     return pl.pallas_call(
         mix_kernel,
-        in_specs=[VMEM] * 5,
+        in_specs=[VMEM] * 6,
         out_specs=(VMEM,) * 3,
         out_shape=(
             out_of((count, width), BF16),
@@ -304,7 +277,7 @@
         ),
         name="mix",
         compiler_params=budget(24576),
-    )(returned, scale, place_first, place_low, place_high)
+    )(returned, stats, scale, place_first, place_low, place_high)
 
 
 def solution(mesh):

time: 100 us -> 93.4 us (0.934)
  blocking collectives: 80.2 us -> 40.8 us
  starting transfers between devices: 1.92 us -> 22.3 us
  waiting for transfers between devices: 0.01 us -> 15.1 us
  Pallas kernels: 15 us -> 12 us
    all_to_all x2 -> x0, blocking collectives: 80.2 us -> none  [the longest x1 46.1 us: per_device(): lax.all_to_all(filled, 'expert', split_axis=0, concat_axis=0, tiled=True)]
    psum x0 -> x3, blocking collectives: none -> 40.8 us  [per_device(): stats = lax.psum(stats, 'dp', axis_index_groups=groups)]
    all_to_all x0 -> x2, starting transfers between devices: none -> 22.3 us  [the longest x1 16.7 us: per_device(): lax.all_to_all(buffer, 'expert', split_axis=0, concat_axis=0, tiled=True)]
    all_to_all x0 -> x2, waiting for transfers between devices: none -> 15.1 us  [the longest x1 15.1 us: per_device(): lax.all_to_all(buffer, 'expert', split_axis=0, concat_axis=0, tiled=True)]
    pallas_call x5 -> x3, Pallas kernels: 11.8 us -> 8.8 us  [the longest x1 7.36 us: per_device(): pl.pallas_call(ffn_kernel, in_specs=[VMEM, HBM, HBM], out_specs=(VMEM, VM...]
    ppermute x1 -> x0, starting transfers between devices: 1.92 us -> none  [per_device(): other = lax.ppermute(group, ('dp', 'expert'), swap)]
  transfers between devices with their start and end apart: 1 -> 2, of which waited for: 0 -> 1; matrix products, arithmetic and copies ran while one was open for 0% -> 0% of each run, Pallas kernels for 11% -> 0%
where the time goes in v3:
time: 93.4 us; the launch traced here: 93 us
  blocking collectives  40.8 us (44%)
  starting transfers between devices  22.3 us (24%)
  waiting for transfers between devices  15.1 us (16%)
  Pallas kernels  12 us (13%)
  local copies, waits for them, and re-layouts  2.05 us (2%)
    psum x3, blocking collectives, per_device(): stats = lax.psum(stats, 'dp', axis_index_groups=groups)  40.8 us
    all_to_all x1, starting transfers between devices, per_device(): lax.all_to_all(buffer, 'expert', split_axis=0, concat_axis=0, tiled=True)  16.7 us
    all_to_all x1, waiting for transfers between devices, per_device(): lax.all_to_all(buffer, 'expert', split_axis=0, concat_axis=0, tiled=True)  15.1 us
    pallas_call x1, Pallas kernels, per_device(): pl.pallas_call(ffn_kernel, in_specs=[VMEM, HBM, HBM], out_specs=(VMEM, VM...  7.36 us
    all_to_all x1, starting transfers between devices, per_device(): lax.all_to_all(computed, 'expert', split_axis=0, concat_axis=0, tiled=True)  5.58 us
    pallas_call x1, Pallas kernels, per_device(): pl.pallas_call(send_kernel, in_specs=[HBM] * 5, out_specs=(VMEM, VMEM), o...  3.2 us
    unnamed x6, local copies, waits for them, and re-layouts  2.05 us
  transfers between devices with their start and end apart: 2, of which 1 were waited for; matrix products, arithmetic and copies ran while one was open for 0% of the time, Pallas kernels for 0%

profile of v3, /device:TPU:2, one launch (start us, length us, event | category | flops | bytes accessed | tf_op | source)
XLA Modules:
  0.0 93.0 jit_solution(17745632428592529466)
XLA Ops:
  0.6 3.2 %send.1 = (bf16[32,13,8,128]{3,2,1,0:T(8,128)(2,1)}, f32[8,256]{1,0:T(8,128)}) custom-call(bf16[256,1024]{1,0:T(8,128)(2,1)} %tokens_hbm.1, bf16[32,1024]{1,0:T(8,128)(2,1)} %bitcast.1, s32[256]{0:T(256)} %assign.1, s32[256]{0:T(256)} %slot.1, s32[256]{0:T(256)} %modality_hbm.1), custom_call_target="tpu_custom_call" | custom-call | tf_op jit(solution)/shard_map/send/pallas_call | solution.py:218
  3.8 16.7 %all-to-all-start = ((bf16[32,13,8,128]{3,2,1,0:T(8,128)(2,1)}), bf16[32,13,8,128]{3,2,1,0:T(8,128)(2,1)S(1)}, u32[]{:S(2)}, u32[]{:S(2)}) async-start(bf16[32,13,8,128]{3,2,1,0:T(8,128)(2,1)} %get-tuple-element.16), calls=%async_computation | async-start | bytes 1703936 | tf_op jit(solution)/shard_map/all_to_all | solution.py:234
  20.6 0.0 copy-start
  20.6 0.7 copy-done
  21.3 0.0 copy-start.1
  21.3 0.7 copy-done.1
  22.0 0.0 copy-start.2
  22.0 0.7 copy-done.2
  22.6 0.2 place.1
  22.9 15.1 %all-to-all-done.received = bf16[32,13,8,128]{3,2,1,0:T(8,128)(2,1)S(1)} async-done(((bf16[32,13,8,128]{3,2,1,0:T(8,128)(2,1)}), bf16[32,13,8,128]{3,2,1,0:T(8,128)(2,1)S(1)}, u32[]{:S(2)}, u32[]{:S(2)}) %all-to-all-start) | async-done | bytes 852000 | tf_op jit(solution)/shard_map/all_to_all | solution.py:234
  38.0 7.4 %ffn.1 = (bf16[32,12,8,128]{3,2,1,0:T(8,128)(2,1)}, f32[8,128]{1,0:T(8,128)S(1)}) custom-call(bf16[32,13,8,128]{3,2,1,0:T(8,128)(2,1)S(1)} %all-to-all-done.received, bf16[1,1024,2048]{2,1,0:T(8,128)(2,1)} %in_hbm.1, bf16[1,2048,1024]{2,1,0:T(8,128)(2,1)} %out_hbm.1), custom_call_target="tpu_custom_call" | custom-call | tf_op jit(solution)/shard_map/ffn/pallas_call | solution.py:247
  45.3 5.6 %all-to-all-start.1 = ((bf16[32,12,8,128]{3,2,1,0:T(8,128)(2,1)}), bf16[32,12,8,128]{3,2,1,0:T(8,128)(2,1)S(1)}, u32[]{:S(2)}, u32[]{:S(2)}) async-start(bf16[32,12,8,128]{3,2,1,0:T(8,128)(2,1)} %get-tuple-element.23), calls=%async_computation.1 | async-start | bytes 1572864 | tf_op jit(solution)/shard_map/all_to_all | solution.py:263
  50.9 2.5 %psum.21 = f32[8,128]{1,0:T(8,128)S(1)} all-reduce(f32[8,128]{1,0:T(8,128)S(1)} %get-tuple-element.24), channel_id=1, replica_groups={{0,32},{64,96},{128,160},{192,224},{256,288},{320,352},{384,416},{448,4..., use_global_device_ids=true, to_apply=%region_0.0 | all-reduce | flops 1024 | bytes 8192 | tf_op jit(solution)/shard_map/psum | solution.py:268
  53.4 14.3 %psum.22 = f32[8,128]{1,0:T(8,128)S(1)} all-reduce(f32[8,128]{1,0:T(8,128)S(1)} %psum.21), channel_id=1, replica_groups={{0,64,128,192},{32,96,160,224},{256,320,384,448},{288,352,416,480},{512..., use_global_device_ids=true, to_apply=%region_1.0 | all-reduce | flops 1024 | bytes 8192 | tf_op jit(solution)/shard_map/psum | solution.py:268
  67.7 24.0 %psum.23.sums = f32[8,128]{1,0:T(8,128)S(1)} all-reduce(f32[8,128]{1,0:T(8,128)S(1)} %psum.22), channel_id=1, replica_groups={{0,256,512,768},{32,288,544,800},{64,320,576,832},{96,352,608,864},{128..., use_global_device_ids=true, to_apply=%region_2.0 | all-reduce | flops 1024 | bytes 8192 | tf_op jit(solution)/shard_map/psum | solution.py:268
  91.7 0.0 all-to-all-done.1.returned
  91.7 1.2 %mix.1 = (bf16[256,1024]{1,0:T(8,128)(2,1)}, f32[2,32]{1,0:T(2,128)}, f32[2,2]{1,0:T(2,128)}) custom-call(bf16[32,12,8,128]{3,2,1,0:T(8,128)(2,1)S(1)} %all-to-all-done.1.returned, f32[8,128]{1,0:T(8,128)S(1)} %psum.23.sums, f32[256,128]{1,0:T(8,128)S(1)} %get-tuple-element.25.gate, bf16[256,256]{1,0:T(8,128)(2,1)S(1)} %get-tuple-element.26.place_first, ...), custom_call_target="tpu_custom_call" | custom-call | tf_op jit(solution)/shard_map/mix/pallas_call | solution.py:269
Async XLA Ops:
  3.8 34.1 %all-to-all-start = ((bf16[32,13,8,128]{3,2,1,0:T(8,128)(2,1)}), bf16[32,13,8,128]{3,2,1,0:T(8,128)(2,1)S(1)}, u32[]{:S(2)}, u32[]{:S(2)}) async-start(bf16[32,13,8,128]{3,2,1,0:T(8,128)(2,1)} %get-tuple-element.16), calls=%async_computation | async-start | bytes 1703936 | tf_op jit(solution)/shard_map/all_to_all | solution.py:234
  20.6 0.7 copy-start
  21.3 0.7 copy-start.1
  22.0 0.7 copy-start.2
  45.3 46.4 %all-to-all-start.1 = ((bf16[32,12,8,128]{3,2,1,0:T(8,128)(2,1)}), bf16[32,12,8,128]{3,2,1,0:T(8,128)(2,1)S(1)}, u32[]{:S(2)}, u32[]{:S(2)}) async-start(bf16[32,12,8,128]{3,2,1,0:T(8,128)(2,1)} %get-tuple-element.23), calls=%async_computation.1 | async-start | bytes 1572864 | tf_op jit(solution)/shard_map/all_to_all | solution.py:263

commit v4 on v3

--- a/solution.py
+++ b/solution.py
@@ -51,8 +51,13 @@
     return copies
 
 
+def piece(source, target, start, size, sem):
+    part = pl.ds(start, size)
+    return pltpu.make_async_copy(source.at[:, part], target.at[:, part], sem)
+
+
 def send_kernel(
-    tokens_hbm, router_hbm, assign_hbm, slot_hbm, modality_hbm, out, gate_out, tokens, router, assign, slot, modality, sems
+    tokens_hbm, router_hbm, assign_hbm, slot_hbm, modality_hbm, out_hbm, gate_out, tokens, router, assign, slot, modality, out, sems, out_sems
 ):
     copies = fetch(
         (assign_hbm, slot_hbm, tokens_hbm, router_hbm, modality_hbm), (assign, slot, tokens, router, modality), sems
@@ -71,13 +76,17 @@
     pick_low = (low == row).astype(BF16)
     pick_high = (high == row).astype(BF16)
     copies[2].wait()
-    main = mm(pick_first, tokens[...]).astype(BF16)
     rest = mm(pick_low, tokens[:, :half]) + mm(pick_high, tokens[:, half:])
     rest = rest.astype(BF16)
+    for t in range(4):
+        out[:, 8 + t] = rest[:, t * LANES : (t + 1) * LANES].reshape(n_expert, ROWS, LANES)
+    back = [piece(out, out_hbm, 8, 4, out_sems.at[0])]
+    back[0].start()
+    main = mm(pick_first, tokens[...]).astype(BF16)
     for t in range(8):
         out[:, t] = main[:, t * LANES : (t + 1) * LANES].reshape(n_expert, ROWS, LANES)
-    for t in range(4):
-        out[:, 8 + t] = rest[:, t * LANES : (t + 1) * LANES].reshape(n_expert, ROWS, LANES)
+    back.append(piece(out, out_hbm, 0, 8, out_sems.at[1]))
+    back[1].start()
     copies[3].wait()
     copies[4].wait()
     logits = mm_t(router[...], tokens[...])
@@ -97,6 +106,10 @@
     hi, mid, lo = split3(terms)
     sums = (mm_t(kinds, hi) + mm_t(kinds, mid) + mm_t(kinds, lo))[:ROWS]
     out[:, 12] = jnp.broadcast_to(stats_tile(sums)[None], (n_expert, ROWS, LANES))
+    back.append(piece(out, out_hbm, 12, 1, out_sems.at[2]))
+    back[2].start()
+    for c in back:
+        c.wait()
 
 
 def total_of(tiles):
@@ -108,7 +121,12 @@
     return jnp.transpose(jnp.broadcast_to(row, (LANES, count)))
 
 
-def place_kernel(gate, assign, slot, scale, place_first, place_low, place_high):
+EARLY = 768
+
+
+def place_kernel(gate, assign, slot, in_hbm, scale, place_first, place_low, place_high, early, sem):
+    ahead = pltpu.make_async_copy(in_hbm.at[0, :, pl.ds(0, EARLY)], early, sem)
+    ahead.start()
     count = gate.shape[1]
     wide = place_first.shape[1]
     first, low, high = pick_labels(assign[...].reshape(1, count), slot[...].reshape(1, count))
@@ -122,22 +140,26 @@
     place_first[...] = (spread(first) == lane).astype(BF16)
     place_low[...] = (spread(low) == lane).astype(BF16)
     place_high[...] = (spread(high) == lane).astype(BF16)
+    ahead.wait()
 
 
 STEP = 512
 
 
-def ffn_kernel(received, in_hbm, out_hbm, out, group, w_in, w_out, rows, hidden, rest, sems):
+def ffn_kernel(received, early, in_hbm, out_hbm, back_hbm, group, w_in, w_out, rows, hidden, rest, out, sems, back_sems):
     n_expert = received.shape[0]
     wide = n_expert * ROWS
     quarter = wide // 2
-    width, inner = w_in.shape
+    inner, width = w_out.shape
     half = width // 2
-    n_in, n_out = inner // STEP, width // STEP
-    cut = [pl.ds(j * STEP, STEP) for j in range(max(n_in, n_out))]
+    edges = list(range(EARLY, inner, STEP)) + [inner]
+    if edges[-1] - edges[-2] < STEP:
+        edges.pop(-2)
+    cuts = [pl.ds(lo, hi - lo) for lo, hi in zip(edges, edges[1:])]
+    halves = [pl.ds(0, half), pl.ds(half, half)]
     copies = fetch(
-        [in_hbm.at[0, :, cut[j]] for j in range(n_in)] + [out_hbm.at[0, :, cut[n]] for n in range(n_out)],
-        [w_in.at[:, cut[j]] for j in range(n_in)] + [w_out.at[:, cut[n]] for n in range(n_out)],
+        [in_hbm.at[0, :, c] for c in cuts] + [out_hbm.at[0, :, c] for c in halves],
+        [w_in.at[:, pl.ds(c.start - EARLY, c.size)] for c in cuts] + [w_out.at[:, c] for c in halves],
         sems,
     )
     for t in range(8):
@@ -150,16 +172,22 @@
     rows[wide:, half:] = mm((have == source + 4).astype(BF16), packed).astype(BF16)
     total = total_of(received[:, 12])
     group[...] = jnp.concatenate([total] * (ROWS // 2), axis=0)
-    for j in range(n_in):
+    for lo in range(0, EARLY, STEP):
+        hi = min(lo + STEP, EARLY)
+        hidden[:, lo:hi] = jax.nn.gelu(mm(rows[...], early[:, lo:hi])).astype(BF16)
+    for j, c in enumerate(cuts):
         copies[j].wait()
-        hidden[:, j * STEP : (j + 1) * STEP] = jax.nn.gelu(mm(rows[...], w_in[:, cut[j]])).astype(BF16)
-    for n in range(n_out):
-        copies[n_in + n].wait()
-        result = mm(hidden[...], w_out[:, cut[n]]).astype(BF16)
-        for k in range(STEP // LANES):
-            t = n * (STEP // LANES) + k
-            out[:, t] = result[:wide, k * LANES : (k + 1) * LANES].reshape(n_expert, ROWS, LANES)
-        rest[:, n * STEP : (n + 1) * STEP] = result[wide:]
+        lo, hi = c.start, c.start + c.size
+        hidden[:, lo:hi] = jax.nn.gelu(mm(rows[...], w_in[:, lo - EARLY : hi - EARLY])).astype(BF16)
+    back = []
+    for n, c in enumerate(halves):
+        copies[len(cuts) + n].wait()
+        result = mm(hidden[...], w_out[:, c]).astype(BF16)
+        for k in range(half // LANES):
+            out[:, 4 * n + k] = result[:wide, k * LANES : (k + 1) * LANES].reshape(n_expert, ROWS, LANES)
+        rest[:, n * half : (n + 1) * half] = result[wide:]
+        back.append(piece(out, back_hbm, 4 * n, 4, back_sems.at[n]))
+        back[n].start()
     want = iota((wide, quarter), 0)
     have = iota((wide, quarter), 1)
     inside = want % 8
@@ -169,9 +197,13 @@
     packed = (mm(to_low, rest[:, :half]) + mm(to_high, rest[:, half:])).astype(BF16)
     for t in range(4):
         out[:, 8 + t] = packed[:, t * LANES : (t + 1) * LANES].reshape(n_expert, ROWS, LANES)
-
-
-def mix_kernel(returned, sums, gate, place_first, place_low, place_high, mixed, importance, entropies):
+    back.append(piece(out, back_hbm, 8, 4, back_sems.at[2]))
+    back[2].start()
+    for c in back:
+        c.wait()
+
+
+def mix_kernel(returned, sums, gate, place_first, place_low, place_high, mixed_hbm, importance, entropies, mixed, sems):
     n_expert = returned.shape[0]
     wide = n_expert * ROWS
     width = mixed.shape[1]
@@ -182,8 +214,12 @@
     packed = jnp.concatenate([returned[:, 8 + t].reshape(wide, LANES) for t in range(4)], axis=1)
     chosen = mm(place_first[...], main[:, :half]) + mm(place_low[...], packed)
     mixed[:, :half] = (scale * chosen).astype(BF16)
+    cuts = [pl.ds(0, half), pl.ds(half, half)]
+    back = [pltpu.make_async_copy(mixed.at[:, c], mixed_hbm.at[:, c], sems.at[i]) for i, c in enumerate(cuts)]
+    back[0].start()
     chosen = mm(place_first[...], main[:, half:]) + mm(place_high[...], packed)
     mixed[:, half:] = (scale * chosen).astype(BF16)
+    back[1].start()
     total = sums[0:2]
     denom = jnp.maximum(total[:, n_expert : n_expert + 1], 1.0)
     mean = total[:, :n_expert] / denom
@@ -192,6 +228,8 @@
     spread = -jnp.sum(terms, axis=1, keepdims=True)
     token = total[:, n_expert + 1 : n_expert + 2] / denom
     entropies[...] = jnp.where(iota((2, 2), 1) == 0, token, spread)
+    for c in back:
+        c.wait()
 
 
 def budget(kib):
@@ -218,7 +256,7 @@
     buffer, gate = pl.pallas_call(
         send_kernel,
         in_specs=[HBM] * 5,
-        out_specs=(VMEM, VMEM),
+        out_specs=(HBM, VMEM),
         out_shape=(block, out_of((ROWS, count), F32)),
         scratch_shapes=[
             pltpu.VMEM((count, width), BF16),
@@ -226,40 +264,42 @@
             ints,
             ints,
             ints,
+            pltpu.VMEM((n_expert, tiles + 1, ROWS, LANES), BF16),
             pltpu.SemaphoreType.DMA((5,)),
+            pltpu.SemaphoreType.DMA((3,)),
         ],
         name="send",
         compiler_params=budget(65472),
     )(tokens, router.T, assign, slot, modality)
     received = lax.all_to_all(buffer, "expert", split_axis=0, concat_axis=0, tiled=True)
     place = out_of((count, wide), BF16)
-    scale, place_first, place_low, place_high = pl.pallas_call(
+    scale, place_first, place_low, place_high, early = pl.pallas_call(
         place_kernel,
-        in_specs=[VMEM] * 3,
-        out_specs=(VMEM,) * 4,
-        out_shape=(out_of((count, LANES), F32), place, place, place),
+        in_specs=[VMEM] * 3 + [HBM],
+        out_specs=(VMEM,) * 5,
+        out_shape=(out_of((count, LANES), F32), place, place, place, out_of((width, EARLY), BF16)),
+        scratch_shapes=[pltpu.SemaphoreType.DMA(())],
         name="place",
         compiler_params=budget(24576),
-    )(gate, assign, slot)
-    received, scale, place_first, place_low, place_high = lax.optimization_barrier(
-        (received, scale, place_first, place_low, place_high)
-    )
+    )(gate, assign, slot, w_in)
     computed, stats = pl.pallas_call(
         ffn_kernel,
-        in_specs=[VMEM, HBM, HBM],
-        out_specs=(VMEM, VMEM),
+        in_specs=[VMEM, VMEM, HBM, HBM],
+        out_specs=(HBM, VMEM),
         out_shape=(out_of((n_expert, tiles, ROWS, LANES), BF16), out_of((ROWS, LANES), F32)),
         scratch_shapes=[
-            pltpu.VMEM((width, inner), BF16),
+            pltpu.VMEM((width, inner - EARLY), BF16),
             pltpu.VMEM((inner, width), BF16),
             pltpu.VMEM((wide * 3 // 2, width), BF16),
             pltpu.VMEM((wide * 3 // 2, inner), BF16),
             pltpu.VMEM((wide // 2, width), BF16),
-            pltpu.SemaphoreType.DMA((inner // STEP + width // STEP,)),
+            pltpu.VMEM((n_expert, tiles, ROWS, LANES), BF16),
+            pltpu.SemaphoreType.DMA((8,)),
+            pltpu.SemaphoreType.DMA((3,)),
         ],
         name="ffn",
         compiler_params=budget(50000),
-    )(received, w_in, w_out)
+    )(received, early, w_in, w_out)
     returned = lax.all_to_all(computed, "expert", split_axis=0, concat_axis=0, tiled=True)
     pairs = [[2 * z, 2 * z + 1] for z in range(n_dp // 2)]
     near = [[8 * j + 2 * z + c for z in range(4)] for j in range(n_dp // 8) for c in range(2)]
@@ -269,12 +309,13 @@
     return pl.pallas_call(
         mix_kernel,
         in_specs=[VMEM] * 6,
-        out_specs=(VMEM,) * 3,
+        out_specs=(HBM, VMEM, VMEM),
         out_shape=(
             out_of((count, width), BF16),
             out_of((2, n_expert), F32),
             out_of((2, 2), F32),
         ),
+        scratch_shapes=[pltpu.VMEM((count, width), BF16), pltpu.SemaphoreType.DMA((2,))],
         name="mix",
         compiler_params=budget(24576),
     )(returned, stats, scale, place_first, place_low, place_high)

time: 93.4 us -> 94 us (level)
  waiting for transfers between devices: 15.1 us -> 12.7 us
  local copies, waits for them, and re-layouts: 2.05 us -> 4.24 us
    all_to_all x1, waiting for transfers between devices: 15.1 us -> 12.7 us  [per_device(): lax.all_to_all(buffer, 'expert', split_axis=0, concat_axis=0, tiled=True)]
    unnamed x6 -> x8, local copies, waits for them, and re-layouts: 2.05 us -> 4.24 us
where the time goes in v4:
time: 94 us; the launch traced here: 93.5 us
  blocking collectives  40.8 us (43%)
  starting transfers between devices  22.3 us (24%)
  Pallas kernels  12.8 us (14%)
  waiting for transfers between devices  12.7 us (14%)
  local copies, waits for them, and re-layouts  4.24 us (5%)
    psum x3, blocking collectives, per_device(): stats = lax.psum(stats, 'dp', axis_index_groups=groups)  40.8 us
    all_to_all x1, starting transfers between devices, per_device(): lax.all_to_all(buffer, 'expert', split_axis=0, concat_axis=0, tiled=True)  16.7 us
    all_to_all x1, waiting for transfers between devices, per_device(): lax.all_to_all(buffer, 'expert', split_axis=0, concat_axis=0, tiled=True)  12.7 us
    pallas_call x1, Pallas kernels, per_device(): pl.pallas_call(ffn_kernel, in_specs=[VMEM, VMEM, HBM, HBM], out_specs=(HB...  7.11 us
    all_to_all x1, starting transfers between devices, per_device(): lax.all_to_all(computed, 'expert', split_axis=0, concat_axis=0, tiled=True)  5.58 us
    unnamed x8, local copies, waits for them, and re-layouts  4.24 us
    pallas_call x1, Pallas kernels, per_device(): pl.pallas_call(send_kernel, in_specs=[HBM] * 5, out_specs=(HBM, VMEM), ou...  3.54 us
  transfers between devices with their start and end apart: 2, of which 1 were waited for; matrix products, arithmetic and copies ran while one was open for 0% of the time, Pallas kernels for 0%

profile of v4, /device:TPU:2, one launch (start us, length us, event | category | flops | bytes accessed | tf_op | source)
XLA Modules:
  0.0 93.5 jit_solution(15050273728246972851)
XLA Ops:
  0.6 3.5 %send.1 = (bf16[32,13,8,128]{3,2,1,0:T(8,128)(2,1)}, f32[8,256]{1,0:T(8,128)}) custom-call(bf16[256,1024]{1,0:T(8,128)(2,1)} %tokens_hbm.1, bf16[32,1024]{1,0:T(8,128)(2,1)} %bitcast.1, s32[256]{0:T(256)} %assign.1, s32[256]{0:T(256)} %slot.1, s32[256]{0:T(256)} %modality_hbm.1), custom_call_target="tpu_custom_call" | custom-call | tf_op jit(solution)/shard_map/send/pallas_call | solution.py:256
  4.2 16.7 %all-to-all-start = ((bf16[32,13,8,128]{3,2,1,0:T(8,128)(2,1)}), bf16[32,13,8,128]{3,2,1,0:T(8,128)(2,1)S(1)}, u32[]{:S(2)}, u32[]{:S(2)}) async-start(bf16[32,13,8,128]{3,2,1,0:T(8,128)(2,1)} %get-tuple-element.12), calls=%async_computation | async-start | bytes 1703936 | tf_op jit(solution)/shard_map/all_to_all | solution.py:274
  20.9 0.0 copy-start
  20.9 2.2 %copy-done = bf16[1,1024,2048]{2,1,0:T(8,128)(2,1)S(1)} copy-done((bf16[1,1024,2048]{2,1,0:T(8,128)(2,1)S(1)}, bf16[1,1024,2048]{2,1,0:T(8,128)(2,1)}, u32[]{:S(2)}) %copy-start) | copy-done | bytes 4194328
  23.1 0.0 copy-start.1
  23.1 0.7 copy-done.1
  23.8 0.0 copy-start.2
  23.8 0.7 copy-done.2
  24.5 0.0 copy-start.3
  24.5 0.7 copy-done.3
  25.2 0.4 place.1
  25.6 12.7 %all-to-all-done.received = bf16[32,13,8,128]{3,2,1,0:T(8,128)(2,1)S(1)} async-done(((bf16[32,13,8,128]{3,2,1,0:T(8,128)(2,1)}), bf16[32,13,8,128]{3,2,1,0:T(8,128)(2,1)S(1)}, u32[]{:S(2)}, u32[]{:S(2)}) %all-to-all-start) | async-done | bytes 852000 | tf_op jit(solution)/shard_map/all_to_all | solution.py:274
  38.3 7.1 %ffn.1 = (bf16[32,12,8,128]{3,2,1,0:T(8,128)(2,1)}, f32[8,128]{1,0:T(8,128)S(1)}) custom-call(bf16[32,13,8,128]{3,2,1,0:T(8,128)(2,1)S(1)} %all-to-all-done.received, bf16[1024,768]{1,0:T(8,128)(2,1)S(1)} %get-tuple-element.14.early, bf16[1,1024,2048]{2,1,0:T(8,128)(2,1)} %in_hbm.3, bf16[1,2048,1024]{2,1,0:T(8,128)(2,1)} %out_hbm.1), custom_call_target="tpu_custom_call" | custom-call | tf_op jit(solution)/shard_map/ffn/pallas_call | solution.py:285
  45.4 5.6 %all-to-all-start.1 = ((bf16[32,12,8,128]{3,2,1,0:T(8,128)(2,1)}), bf16[32,12,8,128]{3,2,1,0:T(8,128)(2,1)S(1)}, u32[]{:S(2)}, u32[]{:S(2)}) async-start(bf16[32,12,8,128]{3,2,1,0:T(8,128)(2,1)} %get-tuple-element.15), calls=%async_computation.1 | async-start | bytes 1572864 | tf_op jit(solution)/shard_map/all_to_all | solution.py:303
  51.0 2.5 %psum.21 = f32[8,128]{1,0:T(8,128)S(1)} all-reduce(f32[8,128]{1,0:T(8,128)S(1)} %get-tuple-element.16), channel_id=1, replica_groups={{0,32},{64,96},{128,160},{192,224},{256,288},{320,352},{384,416},{448,4..., use_global_device_ids=true, to_apply=%region_0.0 | all-reduce | flops 1024 | bytes 8192 | tf_op jit(solution)/shard_map/psum | solution.py:308
  53.5 14.3 %psum.22 = f32[8,128]{1,0:T(8,128)S(1)} all-reduce(f32[8,128]{1,0:T(8,128)S(1)} %psum.21), channel_id=1, replica_groups={{0,64,128,192},{32,96,160,224},{256,320,384,448},{288,352,416,480},{512..., use_global_device_ids=true, to_apply=%region_1.0 | all-reduce | flops 1024 | bytes 8192 | tf_op jit(solution)/shard_map/psum | solution.py:308
  67.8 24.0 %psum.23.sums = f32[8,128]{1,0:T(8,128)S(1)} all-reduce(f32[8,128]{1,0:T(8,128)S(1)} %psum.22), channel_id=1, replica_groups={{0,256,512,768},{32,288,544,800},{64,320,576,832},{96,352,608,864},{128..., use_global_device_ids=true, to_apply=%region_2.0 | all-reduce | flops 1024 | bytes 8192 | tf_op jit(solution)/shard_map/psum | solution.py:308
  91.8 0.0 all-to-all-done.1.returned
  91.8 1.7 %mix.1 = (bf16[256,1024]{1,0:T(8,128)(2,1)}, f32[2,32]{1,0:T(2,128)}, f32[2,2]{1,0:T(2,128)}) custom-call(bf16[32,12,8,128]{3,2,1,0:T(8,128)(2,1)S(1)} %all-to-all-done.1.returned, f32[8,128]{1,0:T(8,128)S(1)} %psum.23.sums, f32[256,128]{1,0:T(8,128)S(1)} %get-tuple-element.17.gate, bf16[256,256]{1,0:T(8,128)(2,1)S(1)} %get-tuple-element.18.place_first, ...), custom_call_target="tpu_custom_call" | custom-call | tf_op jit(solution)/shard_map/mix/pallas_call | solution.py:309
Async XLA Ops:
  4.2 34.1 %all-to-all-start = ((bf16[32,13,8,128]{3,2,1,0:T(8,128)(2,1)}), bf16[32,13,8,128]{3,2,1,0:T(8,128)(2,1)S(1)}, u32[]{:S(2)}, u32[]{:S(2)}) async-start(bf16[32,13,8,128]{3,2,1,0:T(8,128)(2,1)} %get-tuple-element.12), calls=%async_computation | async-start | bytes 1703936 | tf_op jit(solution)/shard_map/all_to_all | solution.py:274
  20.9 2.2 %copy-start = (bf16[1,1024,2048]{2,1,0:T(8,128)(2,1)S(1)}, bf16[1,1024,2048]{2,1,0:T(8,128)(2,1)}, u32[]{:S(2)}) copy-start(bf16[1,1024,2048]{2,1,0:T(8,128)(2,1)} %in_hbm.3) | copy-start | bytes 12582916
  23.1 0.7 copy-start.1
  23.8 0.7 copy-start.2
  24.5 0.7 copy-start.3
  45.4 46.4 %all-to-all-start.1 = ((bf16[32,12,8,128]{3,2,1,0:T(8,128)(2,1)}), bf16[32,12,8,128]{3,2,1,0:T(8,128)(2,1)S(1)}, u32[]{:S(2)}, u32[]{:S(2)}) async-start(bf16[32,12,8,128]{3,2,1,0:T(8,128)(2,1)} %get-tuple-element.15), calls=%async_computation.1 | async-start | bytes 1572864 | tf_op jit(solution)/shard_map/all_to_all | solution.py:303

commit v5 on v4

--- a/solution.py
+++ b/solution.py
@@ -5,6 +5,7 @@
 from jax.experimental.pallas import tpu as pltpu
 from jax.sharding import PartitionSpec as P
 
+
 BOTH = ("dp", "expert")
 F32, BF16, I32 = jnp.float32, jnp.bfloat16, jnp.int32
 LANES = 128
@@ -57,7 +58,7 @@
 
 
 def send_kernel(
-    tokens_hbm, router_hbm, assign_hbm, slot_hbm, modality_hbm, out_hbm, gate_out, tokens, router, assign, slot, modality, out, sems, out_sems
+    tokens_hbm, router_hbm, assign_hbm, slot_hbm, modality_hbm, out, gate_out, tokens, router, assign, slot, modality, sems
 ):
     copies = fetch(
         (assign_hbm, slot_hbm, tokens_hbm, router_hbm, modality_hbm), (assign, slot, tokens, router, modality), sems
@@ -76,17 +77,13 @@
     pick_low = (low == row).astype(BF16)
     pick_high = (high == row).astype(BF16)
     copies[2].wait()
+    main = mm(pick_first, tokens[...]).astype(BF16)
     rest = mm(pick_low, tokens[:, :half]) + mm(pick_high, tokens[:, half:])
     rest = rest.astype(BF16)
+    for t in range(8):
+        out[:, t] = main[:, t * LANES : (t + 1) * LANES].reshape(n_expert, ROWS, LANES)
     for t in range(4):
         out[:, 8 + t] = rest[:, t * LANES : (t + 1) * LANES].reshape(n_expert, ROWS, LANES)
-    back = [piece(out, out_hbm, 8, 4, out_sems.at[0])]
-    back[0].start()
-    main = mm(pick_first, tokens[...]).astype(BF16)
-    for t in range(8):
-        out[:, t] = main[:, t * LANES : (t + 1) * LANES].reshape(n_expert, ROWS, LANES)
-    back.append(piece(out, out_hbm, 0, 8, out_sems.at[1]))
-    back[1].start()
     copies[3].wait()
     copies[4].wait()
     logits = mm_t(router[...], tokens[...])
@@ -106,15 +103,16 @@
     hi, mid, lo = split3(terms)
     sums = (mm_t(kinds, hi) + mm_t(kinds, mid) + mm_t(kinds, lo))[:ROWS]
     out[:, 12] = jnp.broadcast_to(stats_tile(sums)[None], (n_expert, ROWS, LANES))
-    back.append(piece(out, out_hbm, 12, 1, out_sems.at[2]))
-    back[2].start()
-    for c in back:
-        c.wait()
 
 
 def total_of(tiles):
     tile = jnp.sum(tiles.astype(F32), axis=0)
     return (tile[0:2] + tile[2:4]) + tile[4:6]
+
+
+def group_kernel(received, group):
+    total = total_of(received[:, 12])
+    group[...] = jnp.concatenate([total] * (ROWS // 2), axis=0)
 
 
 def column(row, count):
@@ -146,7 +144,7 @@
 STEP = 512
 
 
-def ffn_kernel(received, early, in_hbm, out_hbm, back_hbm, group, w_in, w_out, rows, hidden, rest, out, sems, back_sems):
+def ffn_kernel(received, early, in_hbm, out_hbm, back_hbm, w_in, w_out, rows, hidden, rest, out, sems, back_sems):
     n_expert = received.shape[0]
     wide = n_expert * ROWS
     quarter = wide // 2
@@ -170,8 +168,6 @@
     source = (want // 4) * 8 + want % 4
     rows[wide:, :half] = mm((have == source).astype(BF16), packed).astype(BF16)
     rows[wide:, half:] = mm((have == source + 4).astype(BF16), packed).astype(BF16)
-    total = total_of(received[:, 12])
-    group[...] = jnp.concatenate([total] * (ROWS // 2), axis=0)
     for lo in range(0, EARLY, STEP):
         hi = min(lo + STEP, EARLY)
         hidden[:, lo:hi] = jax.nn.gelu(mm(rows[...], early[:, lo:hi])).astype(BF16)
@@ -203,7 +199,7 @@
         c.wait()
 
 
-def mix_kernel(returned, sums, gate, place_first, place_low, place_high, mixed_hbm, importance, entropies, mixed, sems):
+def mix_kernel(returned, sums, gate, place_first, place_low, place_high, mixed, importance, entropies):
     n_expert = returned.shape[0]
     wide = n_expert * ROWS
     width = mixed.shape[1]
@@ -214,12 +210,8 @@
     packed = jnp.concatenate([returned[:, 8 + t].reshape(wide, LANES) for t in range(4)], axis=1)
     chosen = mm(place_first[...], main[:, :half]) + mm(place_low[...], packed)
     mixed[:, :half] = (scale * chosen).astype(BF16)
-    cuts = [pl.ds(0, half), pl.ds(half, half)]
-    back = [pltpu.make_async_copy(mixed.at[:, c], mixed_hbm.at[:, c], sems.at[i]) for i, c in enumerate(cuts)]
-    back[0].start()
     chosen = mm(place_first[...], main[:, half:]) + mm(place_high[...], packed)
     mixed[:, half:] = (scale * chosen).astype(BF16)
-    back[1].start()
     total = sums[0:2]
     denom = jnp.maximum(total[:, n_expert : n_expert + 1], 1.0)
     mean = total[:, :n_expert] / denom
@@ -228,8 +220,6 @@
     spread = -jnp.sum(terms, axis=1, keepdims=True)
     token = total[:, n_expert + 1 : n_expert + 2] / denom
     entropies[...] = jnp.where(iota((2, 2), 1) == 0, token, spread)
-    for c in back:
-        c.wait()
 
 
 def budget(kib):
@@ -256,7 +246,7 @@
     buffer, gate = pl.pallas_call(
         send_kernel,
         in_specs=[HBM] * 5,
-        out_specs=(HBM, VMEM),
+        out_specs=(VMEM, VMEM),
         out_shape=(block, out_of((ROWS, count), F32)),
         scratch_shapes=[
             pltpu.VMEM((count, width), BF16),
@@ -264,9 +254,7 @@
             ints,
             ints,
             ints,
-            pltpu.VMEM((n_expert, tiles + 1, ROWS, LANES), BF16),
             pltpu.SemaphoreType.DMA((5,)),
-            pltpu.SemaphoreType.DMA((3,)),
         ],
         name="send",
         compiler_params=budget(65472),
@@ -282,11 +270,20 @@
         name="place",
         compiler_params=budget(24576),
     )(gate, assign, slot, w_in)
-    computed, stats = pl.pallas_call(
+    stats = pl.pallas_call(
+        group_kernel,
+        in_specs=[VMEM],
+        out_specs=VMEM,
+        out_shape=out_of((ROWS, LANES), F32),
+        name="group",
+        compiler_params=budget(24576),
+    )(received)
+    other = lax.ppermute(stats, "dp", [(d, d ^ 4) for d in range(n_dp)])
+    matmuls = pl.pallas_call(
         ffn_kernel,
         in_specs=[VMEM, VMEM, HBM, HBM],
-        out_specs=(HBM, VMEM),
-        out_shape=(out_of((n_expert, tiles, ROWS, LANES), BF16), out_of((ROWS, LANES), F32)),
+        out_specs=HBM,
+        out_shape=out_of((n_expert, tiles, ROWS, LANES), BF16),
         scratch_shapes=[
             pltpu.VMEM((width, inner - EARLY), BF16),
             pltpu.VMEM((inner, width), BF16),
@@ -299,23 +296,23 @@
         ],
         name="ffn",
         compiler_params=budget(50000),
-    )(received, early, w_in, w_out)
+    )
+    computed = matmuls(received, early, w_in, w_out)
     returned = lax.all_to_all(computed, "expert", split_axis=0, concat_axis=0, tiled=True)
-    pairs = [[2 * z, 2 * z + 1] for z in range(n_dp // 2)]
-    near = [[8 * j + 2 * z + c for z in range(4)] for j in range(n_dp // 8) for c in range(2)]
-    far = [[8 * j + 2 * z + c for j in range(n_dp // 8)] for z in range(4) for c in range(2)]
-    for groups in (pairs, near, far):
+    near = [[4 * j + i for i in range(4)] for j in range(n_dp // 4)]
+    far = [[8 * j + i for j in range(n_dp // 8)] for i in range(8)]
+    stats = stats + other
+    for groups in (near, far):
         stats = lax.psum(stats, "dp", axis_index_groups=groups)
     return pl.pallas_call(
         mix_kernel,
         in_specs=[VMEM] * 6,
-        out_specs=(HBM, VMEM, VMEM),
+        out_specs=(VMEM,) * 3,
         out_shape=(
             out_of((count, width), BF16),
             out_of((2, n_expert), F32),
             out_of((2, 2), F32),
         ),
-        scratch_shapes=[pltpu.VMEM((count, width), BF16), pltpu.SemaphoreType.DMA((2,))],
         name="mix",
         compiler_params=budget(24576),
     )(returned, stats, scale, place_first, place_low, place_high)

time: 94 us -> 90.4 us (0.962)
  blocking collectives: 40.8 us -> 31.4 us
  starting transfers between devices: 22.3 us -> 28.4 us
  Pallas kernels: 12.8 us -> 10.9 us
  waiting for transfers between devices: 12.7 us -> 14.3 us
    psum x3 -> x2, blocking collectives: 40.8 us -> 31.4 us  [per_device(): stats = lax.psum(stats, 'dp', axis_index_groups=groups)]
    ppermute x0 -> x1, starting transfers between devices: none -> 6.08 us  [per_device(): other = lax.ppermute(stats, 'dp', [(d, d ^ 4) for d in range(n_dp)])]
    pallas_call x3 -> x4, Pallas kernels: 12.4 us -> 10.5 us  [the longest x1 6 us: per_device(): computed = matmuls(received, early, w_in, w_out)]
    ppermute x0 -> x1, waiting for transfers between devices: none -> 1.57 us  [per_device(): other = lax.ppermute(stats, 'dp', [(d, d ^ 4) for d in range(n_dp)])]
  transfers between devices with their start and end apart: 2 -> 3, of which waited for: 1 -> 2; matrix products, arithmetic and copies ran while one was open for 0% -> 0% of each run, Pallas kernels for 0% -> 1%
where the time goes in v5:
time: 90.4 us; the launch traced here: 89.9 us
  blocking collectives  31.4 us (35%)
  starting transfers between devices  28.4 us (31%)
  waiting for transfers between devices  14.3 us (16%)
  Pallas kernels  10.9 us (12%)
  local copies, waits for them, and re-layouts  4.24 us (5%)
    psum x2, blocking collectives, per_device(): stats = lax.psum(stats, 'dp', axis_index_groups=groups)  31.4 us
    all_to_all x1, starting transfers between devices, per_device(): lax.all_to_all(buffer, 'expert', split_axis=0, concat_axis=0, tiled=True)  16.7 us
    all_to_all x1, waiting for transfers between devices, per_device(): lax.all_to_all(buffer, 'expert', split_axis=0, concat_axis=0, tiled=True)  12.7 us
    ppermute x1, starting transfers between devices, per_device(): other = lax.ppermute(stats, 'dp', [(d, d ^ 4) for d in range(n_dp)])  6.08 us
    pallas_call x1, Pallas kernels, per_device(): computed = matmuls(received, early, w_in, w_out)  6 us
    all_to_all x1, starting transfers between devices, per_device(): lax.all_to_all(computed, 'expert', split_axis=0, concat_axis=0, tiled=True)  5.58 us
    unnamed x8, local copies, waits for them, and re-layouts  4.24 us
    pallas_call x1, Pallas kernels, per_device(): pl.pallas_call(send_kernel, in_specs=[HBM] * 5, out_specs=(VMEM, VMEM), o...  3.19 us
  transfers between devices with their start and end apart: 3, of which 2 were waited for; matrix products, arithmetic and copies ran while one was open for 0% of the time, Pallas kernels for 1%

profile of v5, /device:TPU:2, one launch (start us, length us, event | category | flops | bytes accessed | tf_op | source)
XLA Modules:
  0.0 89.9 jit_solution(10145187727043976109)
XLA Ops:
  0.6 3.2 %send.1 = (bf16[32,13,8,128]{3,2,1,0:T(8,128)(2,1)}, f32[8,256]{1,0:T(8,128)}) custom-call(bf16[256,1024]{1,0:T(8,128)(2,1)} %tokens_hbm.1, bf16[32,1024]{1,0:T(8,128)(2,1)} %bitcast.1, s32[256]{0:T(256)} %assign.1, s32[256]{0:T(256)} %slot.1, s32[256]{0:T(256)} %modality_hbm.1), custom_call_target="tpu_custom_call" | custom-call | tf_op jit(solution)/shard_map/send/pallas_call | solution.py:246
  3.8 16.7 %all-to-all-start = ((bf16[32,13,8,128]{3,2,1,0:T(8,128)(2,1)}), bf16[32,13,8,128]{3,2,1,0:T(8,128)(2,1)S(1)}, u32[]{:S(2)}, u32[]{:S(2)}) async-start(bf16[32,13,8,128]{3,2,1,0:T(8,128)(2,1)} %get-tuple-element.10), calls=%async_computation | async-start | bytes 1703936 | tf_op jit(solution)/shard_map/all_to_all | solution.py:262
  20.6 0.0 copy-start
  20.6 2.2 %copy-done = bf16[1,1024,2048]{2,1,0:T(8,128)(2,1)S(1)} copy-done((bf16[1,1024,2048]{2,1,0:T(8,128)(2,1)S(1)}, bf16[1,1024,2048]{2,1,0:T(8,128)(2,1)}, u32[]{:S(2)}) %copy-start) | copy-done | bytes 4194328
  22.8 0.0 copy-start.1
  22.8 0.7 copy-done.1
  23.5 0.0 copy-start.2
  23.5 0.7 copy-done.2
  24.1 0.0 copy-start.3
  24.1 0.7 copy-done.3
  24.8 0.4 place.1
  25.3 12.7 %all-to-all-done.received = bf16[32,13,8,128]{3,2,1,0:T(8,128)(2,1)S(1)} async-done(((bf16[32,13,8,128]{3,2,1,0:T(8,128)(2,1)}), bf16[32,13,8,128]{3,2,1,0:T(8,128)(2,1)S(1)}, u32[]{:S(2)}, u32[]{:S(2)}) %all-to-all-start) | async-done | bytes 852000 | tf_op jit(solution)/shard_map/all_to_all | solution.py:262
  38.0 6.0 %ffn.1 = bf16[32,12,8,128]{3,2,1,0:T(8,128)(2,1)} custom-call(bf16[32,13,8,128]{3,2,1,0:T(8,128)(2,1)S(1)} %all-to-all-done.received, bf16[1024,768]{1,0:T(8,128)(2,1)S(1)} %get-tuple-element.12.early, bf16[1,1024,2048]{2,1,0:T(8,128)(2,1)} %in_hbm.3, bf16[1,2048,1024]{2,1,0:T(8,128)(2,1)} %out_hbm.1), custom_call_target="tpu_custom_call" | custom-call | tf_op jit(solution)/shard_map/ffn/pallas_call | solution.py:300
  44.0 5.6 %all-to-all-start.1 = ((bf16[32,12,8,128]{3,2,1,0:T(8,128)(2,1)}), bf16[32,12,8,128]{3,2,1,0:T(8,128)(2,1)S(1)}, u32[]{:S(2)}, u32[]{:S(2)}) async-start(bf16[32,12,8,128]{3,2,1,0:T(8,128)(2,1)} %ffn.1), calls=%async_computation.1 | async-start | bytes 1572864 | tf_op jit(solution)/shard_map/all_to_all | solution.py:301
  49.6 6.1 %collective-permute-start = (f32[8,128]{1,0:T(8,128)S(1)}, f32[8,128]{1,0:T(8,128)S(1)}, u32[]{:S(2)}, u32[]{:S(2)}) collective-permute-start(f32[8,128]{1,0:T(8,128)S(1)} %group.1), channel_id=1, source_target_pairs={{0,128},{32,160},{64,192},{96,224},{128,0},{160,32},{192,64},{224,... | collective-permute-start | bytes 12296 | tf_op jit(solution)/shard_map/ppermute | solution.py:281
  55.7 1.6 %collective-permute-done = f32[8,128]{1,0:T(8,128)S(1)} collective-permute-done((f32[8,128]{1,0:T(8,128)S(1)}, f32[8,128]{1,0:T(8,128)S(1)}, u32[]{:S(2)}, u32[]{:S(2)}) %collective-permute-start) | collective-permute-done | bytes 4128 | tf_op jit(solution)/shard_map/ppermute | solution.py:281
  57.3 5.9 %psum.14 = f32[8,128]{1,0:T(8,128)S(1)} all-reduce(f32[8,128]{1,0:T(8,128)S(1)} %add.7), channel_id=1, replica_groups={{0,32,64,96},{128,160,192,224},{256,288,320,352},{384,416,448,480},{512..., use_global_device_ids=true, to_apply=%region_0.0 | all-reduce | flops 1024 | bytes 8192 | tf_op jit(solution)/shard_map/psum | solution.py:306
  63.2 25.4 %psum.15.sums = f32[8,128]{1,0:T(8,128)S(1)} all-reduce(f32[8,128]{1,0:T(8,128)S(1)} %psum.14), channel_id=1, replica_groups={{0,256,512,768},{32,288,544,800},{64,320,576,832},{96,352,608,864},{128..., use_global_device_ids=true, to_apply=%region_1.0 | all-reduce | flops 1024 | bytes 8192 | tf_op jit(solution)/shard_map/psum | solution.py:306
  88.6 0.0 all-to-all-done.1.returned
  88.6 1.2 %mix.1 = (bf16[256,1024]{1,0:T(8,128)(2,1)}, f32[2,32]{1,0:T(2,128)}, f32[2,2]{1,0:T(2,128)}) custom-call(bf16[32,12,8,128]{3,2,1,0:T(8,128)(2,1)S(1)} %all-to-all-done.1.returned, f32[8,128]{1,0:T(8,128)S(1)} %psum.15.sums, f32[256,128]{1,0:T(8,128)S(1)} %get-tuple-element.13.gate, bf16[256,256]{1,0:T(8,128)(2,1)S(1)} %get-tuple-element.14.place_first, ...), custom_call_target="tpu_custom_call" | custom-call | tf_op jit(solution)/shard_map/mix/pallas_call | solution.py:307
  (2 shorter events, 0.0 us)
Async XLA Ops:
  3.8 34.1 %all-to-all-start = ((bf16[32,13,8,128]{3,2,1,0:T(8,128)(2,1)}), bf16[32,13,8,128]{3,2,1,0:T(8,128)(2,1)S(1)}, u32[]{:S(2)}, u32[]{:S(2)}) async-start(bf16[32,13,8,128]{3,2,1,0:T(8,128)(2,1)} %get-tuple-element.10), calls=%async_computation | async-start | bytes 1703936 | tf_op jit(solution)/shard_map/all_to_all | solution.py:262
  20.6 2.2 %copy-start = (bf16[1,1024,2048]{2,1,0:T(8,128)(2,1)S(1)}, bf16[1,1024,2048]{2,1,0:T(8,128)(2,1)}, u32[]{:S(2)}) copy-start(bf16[1,1024,2048]{2,1,0:T(8,128)(2,1)} %in_hbm.3) | copy-start | bytes 12582916
  22.8 0.7 copy-start.1
  23.5 0.7 copy-start.2
  24.1 0.7 copy-start.3
  44.0 44.7 %all-to-all-start.1 = ((bf16[32,12,8,128]{3,2,1,0:T(8,128)(2,1)}), bf16[32,12,8,128]{3,2,1,0:T(8,128)(2,1)S(1)}, u32[]{:S(2)}, u32[]{:S(2)}) async-start(bf16[32,12,8,128]{3,2,1,0:T(8,128)(2,1)} %ffn.1), calls=%async_computation.1 | async-start | bytes 1572864 | tf_op jit(solution)/shard_map/all_to_all | solution.py:301
  49.6 7.7 %collective-permute-start = (f32[8,128]{1,0:T(8,128)S(1)}, f32[8,128]{1,0:T(8,128)S(1)}, u32[]{:S(2)}, u32[]{:S(2)}) collective-permute-start(f32[8,128]{1,0:T(8,128)S(1)} %group.1), channel_id=1, source_target_pairs={{0,128},{32,160},{64,192},{96,224},{128,0},{160,32},{192,64},{224,... | collective-permute-start | bytes 12296 | tf_op jit(solution)/shard_map/ppermute | solution.py:281

commit v6 on v5

--- a/solution.py
+++ b/solution.py
@@ -67,8 +67,8 @@
     count, width = tokens.shape
     half = width // 2
     rows = n_expert * ROWS
-    copies[0].wait()
-    copies[1].wait()
+    for i in (0, 1, 3, 4):
+        copies[i].wait()
     experts = assign[...].reshape(1, count)
     slots = slot[...].reshape(1, count)
     first, low, high = pick_labels(experts, slots)
@@ -84,8 +84,6 @@
         out[:, t] = main[:, t * LANES : (t + 1) * LANES].reshape(n_expert, ROWS, LANES)
     for t in range(4):
         out[:, 8 + t] = rest[:, t * LANES : (t + 1) * LANES].reshape(n_expert, ROWS, LANES)
-    copies[3].wait()
-    copies[4].wait()
     logits = mm_t(router[...], tokens[...])
     shifted = logits - jnp.max(logits, axis=0, keepdims=True)
     grown = jnp.exp(shifted)

time: 90.4 us -> 90.1 us (level)
  no operation moved by 1% of the time
where the time goes in v6:
time: 90.1 us; the launch traced here: 89.6 us
  blocking collectives  31.4 us (35%)
  starting transfers between devices  28.4 us (32%)
  waiting for transfers between devices  14.3 us (16%)
  Pallas kernels  10.6 us (12%)
  local copies, waits for them, and re-layouts  4.24 us (5%)
    psum x2, blocking collectives, per_device(): stats = lax.psum(stats, 'dp', axis_index_groups=groups)  31.4 us
    all_to_all x1, starting transfers between devices, per_device(): lax.all_to_all(buffer, 'expert', split_axis=0, concat_axis=0, tiled=True)  16.7 us
    all_to_all x1, waiting for transfers between devices, per_device(): lax.all_to_all(buffer, 'expert', split_axis=0, concat_axis=0, tiled=True)  12.7 us
    ppermute x1, starting transfers between devices, per_device(): other = lax.ppermute(stats, 'dp', [(d, d ^ 4) for d in range(n_dp)])  6.08 us
    pallas_call x1, Pallas kernels, per_device(): computed = matmuls(received, early, w_in, w_out)  6 us
    all_to_all x1, starting transfers between devices, per_device(): lax.all_to_all(computed, 'expert', split_axis=0, concat_axis=0, tiled=True)  5.58 us
    unnamed x8, local copies, waits for them, and re-layouts  4.24 us
    pallas_call x1, Pallas kernels, per_device(): pl.pallas_call(send_kernel, in_specs=[HBM] * 5, out_specs=(VMEM, VMEM), o...  2.9 us
  transfers between devices with their start and end apart: 3, of which 2 were waited for; matrix products, arithmetic and copies ran while one was open for 0% of the time, Pallas kernels for 1%

profile of v6, /device:TPU:2, one launch (start us, length us, event | category | flops | bytes accessed | tf_op | source)
XLA Modules:
  0.0 89.6 jit_solution(12086086961940640606)
XLA Ops:
  0.6 2.9 %send.1 = (bf16[32,13,8,128]{3,2,1,0:T(8,128)(2,1)}, f32[8,256]{1,0:T(8,128)}) custom-call(bf16[256,1024]{1,0:T(8,128)(2,1)} %tokens_hbm.1, bf16[32,1024]{1,0:T(8,128)(2,1)} %bitcast.1, s32[256]{0:T(256)} %assign.1, s32[256]{0:T(256)} %slot.1, s32[256]{0:T(256)} %modality_hbm.1), custom_call_target="tpu_custom_call" | custom-call | tf_op jit(solution)/shard_map/send/pallas_call | solution.py:244
  3.5 16.7 %all-to-all-start = ((bf16[32,13,8,128]{3,2,1,0:T(8,128)(2,1)}), bf16[32,13,8,128]{3,2,1,0:T(8,128)(2,1)S(1)}, u32[]{:S(2)}, u32[]{:S(2)}) async-start(bf16[32,13,8,128]{3,2,1,0:T(8,128)(2,1)} %get-tuple-element.10), calls=%async_computation | async-start | bytes 1703936 | tf_op jit(solution)/shard_map/all_to_all | solution.py:260
  20.3 0.0 copy-start
  20.3 2.2 %copy-done = bf16[1,1024,2048]{2,1,0:T(8,128)(2,1)S(1)} copy-done((bf16[1,1024,2048]{2,1,0:T(8,128)(2,1)S(1)}, bf16[1,1024,2048]{2,1,0:T(8,128)(2,1)}, u32[]{:S(2)}) %copy-start) | copy-done | bytes 4194328
  22.5 0.0 copy-start.1
  22.5 0.7 copy-done.1
  23.2 0.0 copy-start.2
  23.2 0.7 copy-done.2
  23.9 0.0 copy-start.3
  23.9 0.7 copy-done.3
  24.5 0.4 place.1
  25.0 12.7 %all-to-all-done.received = bf16[32,13,8,128]{3,2,1,0:T(8,128)(2,1)S(1)} async-done(((bf16[32,13,8,128]{3,2,1,0:T(8,128)(2,1)}), bf16[32,13,8,128]{3,2,1,0:T(8,128)(2,1)S(1)}, u32[]{:S(2)}, u32[]{:S(2)}) %all-to-all-start) | async-done | bytes 852000 | tf_op jit(solution)/shard_map/all_to_all | solution.py:260
  37.7 6.0 %ffn.1 = bf16[32,12,8,128]{3,2,1,0:T(8,128)(2,1)} custom-call(bf16[32,13,8,128]{3,2,1,0:T(8,128)(2,1)S(1)} %all-to-all-done.received, bf16[1024,768]{1,0:T(8,128)(2,1)S(1)} %get-tuple-element.12.early, bf16[1,1024,2048]{2,1,0:T(8,128)(2,1)} %in_hbm.3, bf16[1,2048,1024]{2,1,0:T(8,128)(2,1)} %out_hbm.1), custom_call_target="tpu_custom_call" | custom-call | tf_op jit(solution)/shard_map/ffn/pallas_call | solution.py:298
  43.7 5.6 %all-to-all-start.1 = ((bf16[32,12,8,128]{3,2,1,0:T(8,128)(2,1)}), bf16[32,12,8,128]{3,2,1,0:T(8,128)(2,1)S(1)}, u32[]{:S(2)}, u32[]{:S(2)}) async-start(bf16[32,12,8,128]{3,2,1,0:T(8,128)(2,1)} %ffn.1), calls=%async_computation.1 | async-start | bytes 1572864 | tf_op jit(solution)/shard_map/all_to_all | solution.py:299
  49.3 6.1 %collective-permute-start = (f32[8,128]{1,0:T(8,128)S(1)}, f32[8,128]{1,0:T(8,128)S(1)}, u32[]{:S(2)}, u32[]{:S(2)}) collective-permute-start(f32[8,128]{1,0:T(8,128)S(1)} %group.1), channel_id=1, source_target_pairs={{0,128},{32,160},{64,192},{96,224},{128,0},{160,32},{192,64},{224,... | collective-permute-start | bytes 12296 | tf_op jit(solution)/shard_map/ppermute | solution.py:279
  55.4 1.6 %collective-permute-done = f32[8,128]{1,0:T(8,128)S(1)} collective-permute-done((f32[8,128]{1,0:T(8,128)S(1)}, f32[8,128]{1,0:T(8,128)S(1)}, u32[]{:S(2)}, u32[]{:S(2)}) %collective-permute-start) | collective-permute-done | bytes 4128 | tf_op jit(solution)/shard_map/ppermute | solution.py:279
  57.0 5.9 %psum.14 = f32[8,128]{1,0:T(8,128)S(1)} all-reduce(f32[8,128]{1,0:T(8,128)S(1)} %add.7), channel_id=1, replica_groups={{0,32,64,96},{128,160,192,224},{256,288,320,352},{384,416,448,480},{512..., use_global_device_ids=true, to_apply=%region_0.0 | all-reduce | flops 1024 | bytes 8192 | tf_op jit(solution)/shard_map/psum | solution.py:304
  62.9 25.4 %psum.15.sums = f32[8,128]{1,0:T(8,128)S(1)} all-reduce(f32[8,128]{1,0:T(8,128)S(1)} %psum.14), channel_id=1, replica_groups={{0,256,512,768},{32,288,544,800},{64,320,576,832},{96,352,608,864},{128..., use_global_device_ids=true, to_apply=%region_1.0 | all-reduce | flops 1024 | bytes 8192 | tf_op jit(solution)/shard_map/psum | solution.py:304
  88.3 0.0 all-to-all-done.1.returned
  88.3 1.2 %mix.1 = (bf16[256,1024]{1,0:T(8,128)(2,1)}, f32[2,32]{1,0:T(2,128)}, f32[2,2]{1,0:T(2,128)}) custom-call(bf16[32,12,8,128]{3,2,1,0:T(8,128)(2,1)S(1)} %all-to-all-done.1.returned, f32[8,128]{1,0:T(8,128)S(1)} %psum.15.sums, f32[256,128]{1,0:T(8,128)S(1)} %get-tuple-element.13.gate, bf16[256,256]{1,0:T(8,128)(2,1)S(1)} %get-tuple-element.14.place_first, ...), custom_call_target="tpu_custom_call" | custom-call | tf_op jit(solution)/shard_map/mix/pallas_call | solution.py:305
  (2 shorter events, 0.0 us)
Async XLA Ops:
  3.5 34.1 %all-to-all-start = ((bf16[32,13,8,128]{3,2,1,0:T(8,128)(2,1)}), bf16[32,13,8,128]{3,2,1,0:T(8,128)(2,1)S(1)}, u32[]{:S(2)}, u32[]{:S(2)}) async-start(bf16[32,13,8,128]{3,2,1,0:T(8,128)(2,1)} %get-tuple-element.10), calls=%async_computation | async-start | bytes 1703936 | tf_op jit(solution)/shard_map/all_to_all | solution.py:260
  20.3 2.2 %copy-start = (bf16[1,1024,2048]{2,1,0:T(8,128)(2,1)S(1)}, bf16[1,1024,2048]{2,1,0:T(8,128)(2,1)}, u32[]{:S(2)}) copy-start(bf16[1,1024,2048]{2,1,0:T(8,128)(2,1)} %in_hbm.3) | copy-start | bytes 12582916
  22.5 0.7 copy-start.1
  23.2 0.7 copy-start.2
  23.9 0.7 copy-start.3
  43.7 44.7 %all-to-all-start.1 = ((bf16[32,12,8,128]{3,2,1,0:T(8,128)(2,1)}), bf16[32,12,8,128]{3,2,1,0:T(8,128)(2,1)S(1)}, u32[]{:S(2)}, u32[]{:S(2)}) async-start(bf16[32,12,8,128]{3,2,1,0:T(8,128)(2,1)} %ffn.1), calls=%async_computation.1 | async-start | bytes 1572864 | tf_op jit(solution)/shard_map/all_to_all | solution.py:299
  49.3 7.7 %collective-permute-start = (f32[8,128]{1,0:T(8,128)S(1)}, f32[8,128]{1,0:T(8,128)S(1)}, u32[]{:S(2)}, u32[]{:S(2)}) collective-permute-start(f32[8,128]{1,0:T(8,128)S(1)} %group.1), channel_id=1, source_target_pairs={{0,128},{32,160},{64,192},{96,224},{128,0},{160,32},{192,64},{224,... | collective-permute-start | bytes 12296 | tf_op jit(solution)/shard_map/ppermute | solution.py:279
